TPU v7x, 128 devices: a whole 4x4x4 slice. The times are simulated.
128 devices in a mesh: group: 2 (over z_hi), tensoror: 4 (over x), seq: 16 (over y, z_lo, core).
Axes of the slice: x: 4, y: 4, z: 4 (z_hi: 2, z_lo: 2; z = z_hi * 2 + z_lo), core: 2. Of those that a mesh axis runs over, the one named last changes fastest.
Arguments:
- visual_hidden: bfloat16 [16, 512, 5120], P('group', 'seq', 'tensoror'), may hold values from -6 to 6
- projector_weight: bfloat16 [5120, 5120], P('tensoror'), may hold values from -0.078125 to 0.078125
- text_embeddings: bfloat16 [16, 2048, 5120], P(('group', 'tensoror'), 'seq'), may hold values from -6 to 6
- tile_counts: int32 [16], replicated, may hold values from 1 to 2, 24 in all
- image_start: int32 [16], replicated, may hold values from 0 to 1536
- norm_gain: float32 [5120], replicated, may hold values from 0.5 to 1.5
- query_weight: bfloat16 [5120, 2560], P('tensoror'), may hold values from -3 to 3
- keyvalue_weight: bfloat16 [5120, 1024], P('tensoror'), may hold values from -0.08385255 to 0.08385255
Outputs:
- context: bfloat16 [16, 2048, 2560], P(('group', 'tensoror'), 'seq')
Inputs may be any that keep to these rules, and one draw needn't show every extreme that they name: `tile_counts`: the counts of all sequences sum to 24.
All inputs are finite; a program needn't handle non-finite values.
Results may differ from a plain program's by a relative error of at most 0.0061.
Values may be sent and summed in bfloat16 or wider, within the bound.
A program may use at most 128 MiB of HBM per device.

v0:
```python
import jax
import jax.numpy as jnp
from jax import lax
from jax.sharding import PartitionSpec as P

QUERY_HEADS = 20
KEY_VALUE_HEADS = 4
HEAD_SIZE = 128
TILE = 256


epsilon = 1e-06
masked_score = -1e30


def shards(
    visual_hidden,
    projector_weight,
    text_embeddings,
    tile_counts,
    image_start,
    norm_gain,
    query_weight,
    keyvalue_weight,
):
    tensor_count = lax.axis_size("tensoror")
    seq_count = lax.axis_size("seq")
    sequence_local, extent_rows, width = text_embeddings.shape
    slot_rows = visual_hidden.shape[1]
    slot_total = slot_rows * seq_count
    query_groups = QUERY_HEADS // KEY_VALUE_HEADS
    tensor_rank = lax.axis_index("tensoror")
    seq_rank = lax.axis_index("seq")
    group_rank = lax.axis_index("group")
    activated = jax.nn.gelu(visual_hidden.astype(jnp.float32), approximate=False).astype(
        jnp.bfloat16
    )
    visual = lax.psum_scatter(
        jnp.dot(activated, projector_weight, preferred_element_type=jnp.float32),
        "tensoror",
        scatter_dimension=0,
        tiled=True,
    ).astype(jnp.bfloat16)
    first_seq = (group_rank * tensor_count + tensor_rank) * sequence_local
    own_counts = lax.dynamic_slice_in_dim(tile_counts, first_seq, sequence_local)
    own_starts = lax.dynamic_slice_in_dim(image_start, first_seq, sequence_local)
    owners = jnp.arange(seq_count, dtype=jnp.int32)
    positions = seq_rank * extent_rows + jnp.arange(extent_rows, dtype=jnp.int32)
    slot_index = positions[None, :] - own_starts[:, None]
    inside = (slot_index >= 0) & (slot_index < TILE * own_counts[:, None])
    first_fill = -(-slot_rows // seq_count)
    held_rows = slot_total // seq_count
    second_fill = -(-extent_rows // seq_count)
    lead = jnp.mod(owners - seq_rank * slot_rows, seq_count)
    pick = lead[:, None] + seq_count * jnp.arange(first_fill, dtype=jnp.int32)[None, :]
    usable = (pick < slot_rows).reshape(-1)
    picked = jnp.take(visual, jnp.clip(pick, 0, slot_rows - 1).reshape(-1), axis=1)
    picked = jnp.where(usable[None, :, None], picked, jnp.zeros((), jnp.bfloat16))
    spread = lax.all_to_all(picked, "seq", split_axis=1, concat_axis=1, tiled=True)
    held_slot = seq_rank + seq_count * jnp.arange(held_rows, dtype=jnp.int32)
    sender = held_slot // slot_rows
    within = held_slot % slot_rows
    turn = (within - jnp.mod(seq_rank - sender * slot_rows, seq_count)) // seq_count
    held = jnp.take(spread, sender * first_fill + turn, axis=1)
    owner_first = -((own_starts[:, None] + seq_rank - owners[None, :] * extent_rows) // seq_count)
    wanted = owner_first[:, :, None] + jnp.arange(second_fill, dtype=jnp.int32)[None, None, :]
    valid = ((wanted >= 0) & (wanted < held_rows)).reshape(sequence_local, seq_count * second_fill)
    wanted = jnp.clip(wanted, 0, held_rows - 1).reshape(sequence_local, seq_count * second_fill)
    sent = jnp.take_along_axis(held, wanted[:, :, None], axis=1)
    sent = jnp.where(valid[:, :, None], sent, jnp.zeros((), jnp.bfloat16))
    arrived = lax.all_to_all(sent, "seq", split_axis=1, concat_axis=1, tiled=True)
    source = jnp.mod(slot_index, seq_count)
    level = jnp.floor_divide(slot_index, seq_count)
    first_at = -((own_starts[:, None] + source - seq_rank * extent_rows) // seq_count)
    row = source * second_fill + jnp.clip(level - first_at, 0, second_fill - 1)
    row = jnp.clip(row, 0, seq_count * second_fill - 1)
    placed = jnp.take_along_axis(arrived, row[:, :, None], axis=1)
    mixed = jnp.where(inside[:, :, None], placed, text_embeddings)
    widened = mixed.astype(jnp.float32)
    mean_square = jnp.mean(widened * widened, axis=-1, keepdims=True)
    normed = (widened * lax.rsqrt(mean_square + epsilon) * norm_gain).astype(jnp.bfloat16)
    token_rows = sequence_local * extent_rows
    flat = normed.reshape(token_rows, width)
    query_cols = query_weight.shape[1]
    pair_cols = keyvalue_weight.shape[1]
    scattered = lax.all_to_all(flat, "tensoror", split_axis=1, concat_axis=0, tiled=True)
    both_sums = lax.psum_scatter(
        jnp.concatenate(
            [
                jnp.dot(scattered, query_weight, preferred_element_type=jnp.float32),
                jnp.dot(scattered, keyvalue_weight, preferred_element_type=jnp.float32),
            ],
            axis=1,
        ),
        "tensoror",
        scatter_dimension=0,
        tiled=True,
    )
    query_totals = both_sums[:, :query_cols]
    pair_sums = both_sums[:, query_cols:]
    query_rows = query_totals.astype(jnp.bfloat16).reshape(
        sequence_local, extent_rows, KEY_VALUE_HEADS, query_groups, HEAD_SIZE
    )
    key_value_rows = pair_sums.astype(jnp.bfloat16).reshape(sequence_local, extent_rows, pair_cols)
    scale = 1.0 / HEAD_SIZE**0.5

    def absorb_block(state_now, device_portion, first_row):
        running_max, denominator, summed = state_now
        portion_rows = device_portion.shape[1]
        divided_pair = device_portion.reshape(
            sequence_local, portion_rows, 2, KEY_VALUE_HEADS, HEAD_SIZE
        )
        keys = divided_pair[:, :, 0]
        values = divided_pair[:, :, 1]
        scores = (
            jnp.einsum("sqkgd,srkd->sqkgr", query_rows, keys, preferred_element_type=jnp.float32)
            * scale
        )
        key_pos = first_row + jnp.arange(portion_rows, dtype=jnp.int32)
        causal_mask = (key_pos[None, :] <= positions[:, None])[None, :, None, None, :]
        scores = jnp.where(causal_mask, scores, masked_score)
        new_max = jnp.maximum(running_max, jnp.max(scores, axis=-1))
        expo = jnp.where(causal_mask, jnp.exp(scores - new_max[..., None]), 0.0)
        rescale = jnp.exp(running_max - new_max)
        denominator = denominator * rescale + jnp.sum(expo, axis=-1)
        added = jnp.einsum(
            "sqkgr,srkd->sqkgd",
            expo.astype(jnp.bfloat16),
            values,
            preferred_element_type=jnp.float32,
        )
        summed = summed * rescale[..., None] + added
        return (new_max, denominator, summed)

    statistic_shape = (sequence_local, extent_rows, KEY_VALUE_HEADS, query_groups)
    starting = (
        jnp.full(statistic_shape, masked_score, jnp.float32),
        jnp.zeros(statistic_shape, jnp.float32),
        jnp.zeros(statistic_shape + (HEAD_SIZE,), jnp.float32),
    )
    device_portion = lax.all_gather(key_value_rows, "seq", axis=1, tiled=True)
    portion_rows = device_portion.shape[1]
    blocks = portion_rows // 512
    stacked = jnp.swapaxes(device_portion.reshape(sequence_local, blocks, 512, pair_cols), 0, 1)
    offsets = 512 * jnp.arange(blocks, dtype=jnp.int32)

    def one_block(state_inner, operands):
        return (absorb_block(state_inner, operands[0], operands[1]), None)

    result, unused = lax.scan(one_block, starting, (stacked, offsets))
    running_max, denominator, summed = result
    context = summed / denominator[..., None]
    return context.astype(jnp.bfloat16).reshape(
        sequence_local, extent_rows, QUERY_HEADS * HEAD_SIZE
    )


def solution(mesh):
    in_specs = (
        P("group", "seq", "tensoror"),
        P("tensoror", None),
        P(("group", "tensoror"), "seq", None),
        P(),
        P(),
        P(),
        P("tensoror", None),
        P("tensoror", None),
    )
    out_specs = P(("group", "tensoror"), "seq", None)
    return jax.shard_map(shards, mesh=mesh, in_specs=in_specs, out_specs=out_specs, check_vma=False)
```

profile of v0, /device:TPU:57, one launch (start us, length us, event | category | flops | bytes accessed | tf_op | source)
XLA Modules:
  0.0 545.1 jit_solution(14165452904315878417)
XLA Ops:
  6.5 13.5 %fusion.15 = f32[8,32,5120]{2,1,0:T(8,128)} fusion(bf16[1280,5120]{1,0:T(8,128)(2,1)} %param.13, bf16[8,32,1280]{2,1,0:T(8,128)(2,1)} %param.12), kind=kOutput, calls=%fused_computation.29 | convolution fusion | flops 3377070080 | bytes 19005440 | tf_op jit(solution)/shard_map/dot_general | solution.py:39
  20.9 56.4 %reduce-scatter.3.cloned.1.call-done = f32[2,32,5120]{2,1,0:T(8,128)} async-done(((f32[8,32,5120]{2,1,0:T(8,128)}), f32[2,32,5120]{2,1,0:T(8,128)}) %reduce-scatter.3.cloned.1.call-update) | async-done | bytes 1310736 | tf_op jit(solution)/shard_map/reduce_scatter | solution.py:38
  80.1 3.0 gather_fusion.2
  84.9 6.5 %all-to-all-start = ((bf16[2,32,5120]{2,0,1:T(2,128)(2,1)}), bf16[2,32,5120]{2,0,1:T(2,128)(2,1)S(1)}, u32[]{:S(2)}, u32[]{:S(2)}) async-start(bf16[2,32,5120]{2,0,1:T(2,128)(2,1)} %broadcast_select_fusion.2), calls=%async_computation.1 | async-start | bytes 1310720 | tf_op jit(solution)/shard_map/all_to_all | solution.py:59
  91.8 7.6 %all-to-all-done = bf16[2,32,5120]{2,0,1:T(2,128)(2,1)S(1)} async-done(((bf16[2,32,5120]{2,0,1:T(2,128)(2,1)}), bf16[2,32,5120]{2,0,1:T(2,128)(2,1)S(1)}, u32[]{:S(2)}, u32[]{:S(2)}) %all-to-all-start) | async-done | bytes 655392 | tf_op jit(solution)/shard_map/all_to_all | solution.py:59
  99.4 2.7 gather_fusion.3
  103.9 10.3 %gather_fusion = bf16[256,5120]{1,0:T(8,128)(2,1)} fusion(bf16[2,32,5120]{2,1,0:T(8,128)(2,1)S(1)} %copy.87, s32[256]{0:T(256)S(1)} %fusion.93), kind=kCustom, calls=%fused_computation.2 | custom fusion | bytes 5244928 | tf_op jit(solution)/shard_map/jit(take_along_axis)/gather | solution.py:69
  114.2 2.1 select_select_fusion.1
  116.4 4.4 copy.88
  120.7 8.2 %all-to-all-start.1 = ((bf16[2,128,5120]{2,0,1:T(2,128)(2,1)}), bf16[2,128,5120]{2,0,1:T(2,128)(2,1)}, u32[]{:S(2)}, u32[]{:S(2)}) async-start(bf16[2,128,5120]{2,0,1:T(2,128)(2,1)} %copy.88), calls=%async_computation.2 | async-start | bytes 5242880 | tf_op jit(solution)/shard_map/all_to_all | solution.py:71
  129.2 30.3 %all-to-all-done.1 = bf16[2,128,5120]{2,0,1:T(2,128)(2,1)} async-done(((bf16[2,128,5120]{2,0,1:T(2,128)(2,1)}), bf16[2,128,5120]{2,0,1:T(2,128)(2,1)}, u32[]{:S(2)}, u32[]{:S(2)}) %all-to-all-start.1) | async-done | bytes 2621472 | tf_op jit(solution)/shard_map/all_to_all | solution.py:71
  159.5 3.8 copy.89
  163.3 8.6 %gather_fusion.1 = bf16[256,5120]{1,0:T(8,128)(2,1)} fusion(bf16[2,128,5120]{2,1,0:T(8,128)(2,1)} %copy.89, s32[256]{0:T(256)S(1)} %fusion.92), kind=kCustom, calls=%fused_computation.3 | custom fusion | bytes 5244928 | tf_op jit(solution)/shard_map/jit(take_along_axis)/gather | solution.py:77
  172.0 3.9 fusion.17
  176.0 3.7 fusion.19
  179.7 6.2 %all_to_all.22 = bf16[256,4,1280]{2,1,0:T(4,128)(2,1)} reshape(bf16[2,128,5120]{2,1,0:T(8,128)(2,1)} %fusion.19) | data formatting | bytes 5242880 | tf_op jit(solution)/shard_map/all_to_all | solution.py:86
  185.9 2.1 copy.90
  188.0 34.2 %all_to_all.29 = bf16[256,4,1280]{2,0,1:T(8,128)(2,1)S(1)} all-to-all(bf16[256,4,1280]{2,0,1:T(8,128)(2,1)S(1)} %copy.90), channel_id=1, replica_groups=mesh['group'=2,'tensoror'=4,'seq'=16] {'tensoror'}, dimensions={1} | all-to-all | bytes 5242880 | tf_op jit(solution)/shard_map/all_to_all | solution.py:86
  222.1 9.1 %fusion.128 = f32[1024,2560]{1,0:T(8,128)S(1)} fusion(bf16[1024,1280]{1,0:T(8,128)(2,1)S(1)} %bitcast.85, bf16[1280,2560]{1,0:T(8,128)(2,1)} %param.18), kind=kOutput, calls=%fused_computation.223 | convolution fusion | flops 6710886400 | bytes 19660800 | tf_op jit(solution)/shard_map/dot_general | solution.py:90
  231.2 2.9 fusion.129
  234.1 5.5 %pad_maximum_fusion = f32[1024,3584]{1,0:T(8,128)} fusion(f32[1024,1024]{1,0:T(8,128)S(1)} %fusion.129, f32[1024,2560]{1,0:T(8,128)S(1)} %fusion.128), kind=kLoop, calls=%fused_computation.28 | loop fusion | flops 3670016 | bytes 29360128 | tf_op jit(solution)/shard_map/concatenate | solution.py:88
  239.7 134.9 %reduce-scatter.5.cloned.1.call-done = f32[256,3584]{1,0:T(8,128)} async-done(((f32[1024,3584]{1,0:T(8,128)}), f32[256,3584]{1,0:T(8,128)}) %reduce-scatter.5.cloned.1.call-update) | async-done | bytes 3670032 | tf_op jit(solution)/shard_map/reduce_scatter | solution.py:87
  374.6 2.2 convert.4
  378.9 3.4 reshape.607
  383.9 45.5 %all-gather.2.cloned.1.call-done = bf16[2,2048,1024]{2,1,0:T(8,128)(2,1)} async-done(((bf16[2,128,1024]{2,1,0:T(8,128)(2,1)}), bf16[2,2048,1024]{2,1,0:T(8,128)(2,1)}) %all-gather.2.cloned.1.call-update) | async-done | bytes 8388624 | tf_op jit(solution)/shard_map/all_gather | solution.py:141
  429.3 103.0 %while.15 = (s32[]{:T(128)}, f32[2,128,4,5]{1,3,2,0:T(8,128)S(1)}, f32[2,128,4,5]{1,3,2,0:T(8,128)S(1)}, f32[2,128,4,5,128]{1,4,3,2,0:T(8,128)}, s32[4]{0:T(128)...) while((s32[]{:T(128)}, f32[2,128,4,5]{1,3,2,0:T(8,128)S(1)}, ...), condition=%wide.region_6.8_spmd.clone, body=%wide.region_3.7_spmd.clone.sunk | while | flops 1378313856 | bytes 99448000 | solution.py:150
  430.8 1.8 constant_dynamic-slice_fusion.2
  432.6 2.5 copy.106
  435.1 7.7 %fusion.142 = (f32[2,128,4,5]{1,3,2,0:T(8,128)S(1)}, f32[2,4,512,128,5]{3,2,4,1,0:T(8,128)}) fusion(pred[128,512]{0,1:T(8,128)(4,1)S(1)} %broadcast_compare_fusion.2, bf16[2,128,4,5,128]{4,1,3,2,0:T(8,128)(2,1)} %get-tuple-element.239, bf16[2,512,2,4,128]{1,4,3,2,0:T(8,128)(2,1)} %bitcast.79), kind=kOutput, calls=%fused_computation.7.clone.1 | convolution fusion | flops 678947840 | bytes 12931072 | tf_op jit(solution)/shard_map/while/body/eval_jaxpr/sqkgd,srkd->sqkgr/dot_general | solution.py:116
  442.8 6.7 %fusion.143 = f32[2,128,4,5]{1,3,2,0:T(8,128)S(1)} fusion(f32[2,4,512,128,5]{3,2,4,1,0:T(8,128)} %get-tuple-element.210, f32[2,128,4,5]{1,3,2,0:T(8,128)S(1)} %select_maximum_fusion.2, pred[128,512]{0,1:T(8,128)(4,1)S(1)} %broadcast_compare_fusion.2), kind=kLoop, calls=%fused_computation.9.clone.1 | loop fusion | flops 13102080 | bytes 10592256 | tf_op jit(solution)/shard_map/while/body/eval_jaxpr/reduce_sum | solution.py:125
  449.8 4.3 bitcast_add_fusion.2
  455.6 1.8 constant_dynamic-slice_fusion.2
  457.3 2.5 copy.106
  459.9 7.7 %fusion.142 = (f32[2,128,4,5]{1,3,2,0:T(8,128)S(1)}, f32[2,4,512,128,5]{3,2,4,1,0:T(8,128)}) fusion(pred[128,512]{0,1:T(8,128)(4,1)S(1)} %broadcast_compare_fusion.2, bf16[2,128,4,5,128]{4,1,3,2,0:T(8,128)(2,1)} %get-tuple-element.239, bf16[2,512,2,4,128]{1,4,3,2,0:T(8,128)(2,1)} %bitcast.79), kind=kOutput, calls=%fused_computation.7.clone.1 | convolution fusion | flops 678947840 | bytes 12931072 | tf_op jit(solution)/shard_map/while/body/eval_jaxpr/sqkgd,srkd->sqkgr/dot_general | solution.py:116
  467.6 6.7 %fusion.143 = f32[2,128,4,5]{1,3,2,0:T(8,128)S(1)} fusion(f32[2,4,512,128,5]{3,2,4,1,0:T(8,128)} %get-tuple-element.210, f32[2,128,4,5]{1,3,2,0:T(8,128)S(1)} %select_maximum_fusion.2, pred[128,512]{0,1:T(8,128)(4,1)S(1)} %broadcast_compare_fusion.2), kind=kLoop, calls=%fused_computation.9.clone.1 | loop fusion | flops 13102080 | bytes 10592256 | tf_op jit(solution)/shard_map/while/body/eval_jaxpr/reduce_sum | solution.py:125
  474.5 5.6 %bitcast_add_fusion.2 = f32[2,128,4,5,128]{1,4,3,2,0:T(8,128)} fusion(f32[2,128,4,5,128]{1,4,3,2,0:T(8,128)} %get-tuple-element.226, f32[2,4,512,128,5]{3,2,4,1,0:T(8,128)S(1)} %copy-done.2, f32[2,128,4,5]{1,3,2,0:T(8,128)S(1)} %select_maximum_fusion.2, pred[128,512]{0,1:T(8,128)(4,1)S(1)} %broadcast_compare_fusion.2, ...), kind=kOutput, calls=%fused_computation.12.clone.1 | convolution fusion | flops 686161920 | bytes 16908288 | tf_op jit(solution)/shard_map/while/body/eval_jaxpr/sqkgr,srkd->sqkgd/dot_general | solution.py:126
  481.6 1.8 constant_dynamic-slice_fusion.2
  483.4 2.5 copy.106
  486.0 7.7 %fusion.142 = (f32[2,128,4,5]{1,3,2,0:T(8,128)S(1)}, f32[2,4,512,128,5]{3,2,4,1,0:T(8,128)}) fusion(pred[128,512]{0,1:T(8,128)(4,1)S(1)} %broadcast_compare_fusion.2, bf16[2,128,4,5,128]{4,1,3,2,0:T(8,128)(2,1)} %get-tuple-element.239, bf16[2,512,2,4,128]{1,4,3,2,0:T(8,128)(2,1)} %bitcast.79), kind=kOutput, calls=%fused_computation.7.clone.1 | convolution fusion | flops 678947840 | bytes 12931072 | tf_op jit(solution)/shard_map/while/body/eval_jaxpr/sqkgd,srkd->sqkgr/dot_general | solution.py:116
  493.7 6.7 %fusion.143 = f32[2,128,4,5]{1,3,2,0:T(8,128)S(1)} fusion(f32[2,4,512,128,5]{3,2,4,1,0:T(8,128)} %get-tuple-element.210, f32[2,128,4,5]{1,3,2,0:T(8,128)S(1)} %select_maximum_fusion.2, pred[128,512]{0,1:T(8,128)(4,1)S(1)} %broadcast_compare_fusion.2), kind=kLoop, calls=%fused_computation.9.clone.1 | loop fusion | flops 13102080 | bytes 10592256 | tf_op jit(solution)/shard_map/while/body/eval_jaxpr/reduce_sum | solution.py:125
  500.6 5.6 %bitcast_add_fusion.2 = f32[2,128,4,5,128]{1,4,3,2,0:T(8,128)} fusion(f32[2,128,4,5,128]{1,4,3,2,0:T(8,128)} %get-tuple-element.226, f32[2,4,512,128,5]{3,2,4,1,0:T(8,128)S(1)} %copy-done.2, f32[2,128,4,5]{1,3,2,0:T(8,128)S(1)} %select_maximum_fusion.2, pred[128,512]{0,1:T(8,128)(4,1)S(1)} %broadcast_compare_fusion.2, ...), kind=kOutput, calls=%fused_computation.12.clone.1 | convolution fusion | flops 686161920 | bytes 16908288 | tf_op jit(solution)/shard_map/while/body/eval_jaxpr/sqkgr,srkd->sqkgd/dot_general | solution.py:126
  507.7 1.8 constant_dynamic-slice_fusion.2
  509.5 2.5 copy.106
  512.0 7.7 %fusion.142 = (f32[2,128,4,5]{1,3,2,0:T(8,128)S(1)}, f32[2,4,512,128,5]{3,2,4,1,0:T(8,128)}) fusion(pred[128,512]{0,1:T(8,128)(4,1)S(1)} %broadcast_compare_fusion.2, bf16[2,128,4,5,128]{4,1,3,2,0:T(8,128)(2,1)} %get-tuple-element.239, bf16[2,512,2,4,128]{1,4,3,2,0:T(8,128)(2,1)} %bitcast.79), kind=kOutput, calls=%fused_computation.7.clone.1 | convolution fusion | flops 678947840 | bytes 12931072 | tf_op jit(solution)/shard_map/while/body/eval_jaxpr/sqkgd,srkd->sqkgr/dot_general | solution.py:116
  519.8 6.7 %fusion.143 = f32[2,128,4,5]{1,3,2,0:T(8,128)S(1)} fusion(f32[2,4,512,128,5]{3,2,4,1,0:T(8,128)} %get-tuple-element.210, f32[2,128,4,5]{1,3,2,0:T(8,128)S(1)} %select_maximum_fusion.2, pred[128,512]{0,1:T(8,128)(4,1)S(1)} %broadcast_compare_fusion.2), kind=kLoop, calls=%fused_computation.9.clone.1 | loop fusion | flops 13102080 | bytes 10592256 | tf_op jit(solution)/shard_map/while/body/eval_jaxpr/reduce_sum | solution.py:125
  526.7 5.6 %bitcast_add_fusion.2 = f32[2,128,4,5,128]{1,4,3,2,0:T(8,128)} fusion(f32[2,128,4,5,128]{1,4,3,2,0:T(8,128)} %get-tuple-element.226, f32[2,4,512,128,5]{3,2,4,1,0:T(8,128)S(1)} %copy-done.2, f32[2,128,4,5]{1,3,2,0:T(8,128)S(1)} %select_maximum_fusion.2, pred[128,512]{0,1:T(8,128)(4,1)S(1)} %broadcast_compare_fusion.2, ...), kind=kOutput, calls=%fused_computation.12.clone.1 | convolution fusion | flops 686161920 | bytes 16908288 | tf_op jit(solution)/shard_map/while/body/eval_jaxpr/sqkgr,srkd->sqkgd/dot_general | solution.py:126
  532.4 3.3 divide_convert_fusion
  535.7 2.4 copy.95
  (102 shorter events, 18.7 us)
Async XLA Ops:
  6.5 224.7 %copy-start = (bf16[1280,1024]{1,0:T(8,128)(2,1)S(1)}, bf16[1280,1024]{1,0:T(8,128)(2,1)}, u32[]{:S(2)}) copy-start(bf16[1280,1024]{1,0:T(8,128)(2,1)} %param.19) | copy-start | bytes 7864324
  6.5 70.7 %reduce-scatter.3.cloned.1.call-start = ((), (), s32[]{:S(2)}) async-start(), calls=%async_computation.5 | async-start | bytes 6553600 | tf_op jit(solution)/shard_map/reduce_scatter | solution.py:38
  20.0 0.7 copy-start.7
  20.0 0.7 copy-start.8
  84.9 14.5 %all-to-all-start = ((bf16[2,32,5120]{2,0,1:T(2,128)(2,1)}), bf16[2,32,5120]{2,0,1:T(2,128)(2,1)S(1)}, u32[]{:S(2)}, u32[]{:S(2)}) async-start(bf16[2,32,5120]{2,0,1:T(2,128)(2,1)} %broadcast_select_fusion.2), calls=%async_computation.1 | async-start | bytes 1310720 | tf_op jit(solution)/shard_map/all_to_all | solution.py:59
  120.7 38.8 %all-to-all-start.1 = ((bf16[2,128,5120]{2,0,1:T(2,128)(2,1)}), bf16[2,128,5120]{2,0,1:T(2,128)(2,1)}, u32[]{:S(2)}, u32[]{:S(2)}) async-start(bf16[2,128,5120]{2,0,1:T(2,128)(2,1)} %copy.88), calls=%async_computation.2 | async-start | bytes 5242880 | tf_op jit(solution)/shard_map/all_to_all | solution.py:71
  128.9 245.7 %reduce-scatter.5.cloned.1.call-start = ((), (), s32[]{:S(2)}) async-start(), calls=%async_computation.6 | async-start | bytes 18350080 | tf_op jit(solution)/shard_map/reduce_scatter | solution.py:87
  163.3 12.5 %copy-start.6 = (f32[5120]{0:T(1024)S(1)}, f32[5120]{0:T(1024)}, u32[]{:S(2)}) copy-start(f32[5120]{0:T(1024)} %param.17) | copy-start | bytes 61444
  171.9 3.9 copy-start.4
  171.9 4.1 copy-start.5
  239.6 189.7 %all-gather.2.cloned.1.call-start = ((), (), s32[]{:S(2)}) async-start(), calls=%async_computation.7 | async-start | bytes 8912896 | tf_op jit(solution)/shard_map/all_gather | solution.py:141
  435.1 14.4 %copy-start.3 = (bf16[1,2,512,1024]{2,3,1,0:T(8,128)(2,1)S(1)}, bf16[1,2,512,1024]{2,3,1,0:T(8,128)(2,1)}, u32[]{:S(2)}) copy-start(bf16[1,2,512,1024]{2,3,1,0:T(8,128)(2,1)} %copy.106) | copy-start | bytes 6291460 | tf_op jit(solution)/shard_map/while
  442.8 7.0 %copy-start.2 = (f32[2,4,512,128,5]{3,2,4,1,0:T(8,128)S(1)}, f32[2,4,512,128,5]{3,2,4,1,0:T(8,128)}, u32[]{:S(2)}) copy-start(f32[2,4,512,128,5]{3,2,4,1,0:T(8,128)} %get-tuple-element.210) | copy-start | bytes 31457284 | tf_op jit(solution)/shard_map/while
  459.9 14.4 %copy-start.3 = (bf16[1,2,512,1024]{2,3,1,0:T(8,128)(2,1)S(1)}, bf16[1,2,512,1024]{2,3,1,0:T(8,128)(2,1)}, u32[]{:S(2)}) copy-start(bf16[1,2,512,1024]{2,3,1,0:T(8,128)(2,1)} %copy.106) | copy-start | bytes 6291460 | tf_op jit(solution)/shard_map/while
  467.6 7.0 %copy-start.2 = (f32[2,4,512,128,5]{3,2,4,1,0:T(8,128)S(1)}, f32[2,4,512,128,5]{3,2,4,1,0:T(8,128)}, u32[]{:S(2)}) copy-start(f32[2,4,512,128,5]{3,2,4,1,0:T(8,128)} %get-tuple-element.210) | copy-start | bytes 31457284 | tf_op jit(solution)/shard_map/while
  486.0 14.4 %copy-start.3 = (bf16[1,2,512,1024]{2,3,1,0:T(8,128)(2,1)S(1)}, bf16[1,2,512,1024]{2,3,1,0:T(8,128)(2,1)}, u32[]{:S(2)}) copy-start(bf16[1,2,512,1024]{2,3,1,0:T(8,128)(2,1)} %copy.106) | copy-start | bytes 6291460 | tf_op jit(solution)/shard_map/while
  493.7 7.0 %copy-start.2 = (f32[2,4,512,128,5]{3,2,4,1,0:T(8,128)S(1)}, f32[2,4,512,128,5]{3,2,4,1,0:T(8,128)}, u32[]{:S(2)}) copy-start(f32[2,4,512,128,5]{3,2,4,1,0:T(8,128)} %get-tuple-element.210) | copy-start | bytes 31457284 | tf_op jit(solution)/shard_map/while
  512.0 14.4 %copy-start.3 = (bf16[1,2,512,1024]{2,3,1,0:T(8,128)(2,1)S(1)}, bf16[1,2,512,1024]{2,3,1,0:T(8,128)(2,1)}, u32[]{:S(2)}) copy-start(bf16[1,2,512,1024]{2,3,1,0:T(8,128)(2,1)} %copy.106) | copy-start | bytes 6291460 | tf_op jit(solution)/shard_map/while
  519.7 7.0 %copy-start.2 = (f32[2,4,512,128,5]{3,2,4,1,0:T(8,128)S(1)}, f32[2,4,512,128,5]{3,2,4,1,0:T(8,128)}, u32[]{:S(2)}) copy-start(f32[2,4,512,128,5]{3,2,4,1,0:T(8,128)} %get-tuple-element.210) | copy-start | bytes 31457284 | tf_op jit(solution)/shard_map/while
  532.4 5.7 %copy-start.1 = (bf16[1280,1024]{1,0:T(8,128)(2,1)S(1)}, bf16[1280,1024]{1,0:T(8,128)(2,1)}, u32[]{:S(2)}) copy-start(bf16[1280,1024]{1,0:T(8,128)(2,1)} %param.19) | copy-start | bytes 7864324
Sparse Core Ops, SparseCore 0:
  20.2 57.0 reduce-scatter.2
  239.7 134.7 reduce-scatter.4
  377.8 51.4 all-gather.1
where the time goes:
time: 555 us; the launch traced here: 545 us
  waiting for transfers between devices  275 us (50%)
  matrix products  77.5 us (14%)
  local copies, waits for them, and re-layouts  73.9 us (13%)
  other arithmetic  56.2 us (10%)
  blocking collectives  34.2 us (6%)
  starting transfers between devices  14.7 us (3%)
  between operations  13.8 us (2%)
    reduce_scatter x1, waiting for transfers between devices, shards(): lax.psum_scatter(jnp.concatenate([jnp.dot(scattered, query_weight, prefer...  135 us
    reduce_scatter x1, waiting for transfers between devices, shards(): lax.psum_scatter(jnp.dot(activated, projector_weight, preferred_element_t...  56.4 us
    all_gather x1, waiting for transfers between devices, shards(): device_portion = lax.all_gather(key_value_rows, 'seq', axis=1, tiled=True)  45.5 us
    all_to_all x1, blocking collectives, shards(): lax.all_to_all(flat, 'tensoror', split_axis=1, concat_axis=0, tiled=True)  34.2 us
    dot_general x4, matrix products, absorb_block(): jnp.einsum('sqkgd,srkd->sqkgr', query_rows, keys, preferred_element_type=...  30.7 us
    all_to_all x1, waiting for transfers between devices, shards(): lax.all_to_all(sent, 'seq', split_axis=1, concat_axis=1, tiled=True)  30.3 us
    reduce_sum x4, other arithmetic, absorb_block(): denominator = denominator * rescale + jnp.sum(expo, axis=-1)  26.7 us
    dot_general x4, matrix products, absorb_block(): jnp.einsum('sqkgr,srkd->sqkgd', expo.astype(jnp.bfloat16), values, prefer...  21.3 us
  transfers between devices with their start and end apart: 5, of which 5 were waited for; matrix products, arithmetic and copies ran while one was open for 1% of the time, Pallas kernels for 0%

commit v1 on v0

v1 whole, which is shorter than its diff:
```python
import functools
import math

import jax
import jax.numpy as jnp
from jax import lax
from jax.experimental import pallas as pl
from jax.experimental.pallas import tpu as pltpu
from jax.sharding import PartitionSpec as P

QUERY_HEADS = 20
KEY_VALUE_HEADS = 4
HEAD_SIZE = 128
TILE = 256
GROUP_HEADS = QUERY_HEADS // KEY_VALUE_HEADS
MESH = pl.DeviceIdType.MESH

epsilon = 1e-06
masked_score = -1e30
VMEM = 60 * 1024 * 1024


def neighbours():
    count = lax.axis_size("tensoror")
    me = lax.axis_index("tensoror")
    return me, lax.rem(me + 1, count), lax.rem(me + 2, count), lax.rem(me + 3, count)


def greet(peers):
    barrier = pltpu.get_barrier_semaphore()
    for peer in peers:
        pl.semaphore_signal(
            barrier, inc=1, device_id={"tensoror": peer}, device_id_type=MESH
        )
    pl.semaphore_wait(barrier, len(peers))


TO_RIGHT = (False, True, True, False, False, True)


def piece(kind, c, send, recv, send_sem, recv_sem):
    me, right, opposite, left = neighbours()
    return pltpu.make_async_remote_copy(
        src_ref=send.at[kind, c],
        dst_ref=recv.at[kind, c],
        send_sem=send_sem.at[kind, c],
        recv_sem=recv_sem.at[kind, c],
        device_id={"tensoror": right if TO_RIGHT[kind] else left},
        device_id_type=MESH,
    )


def first_pieces(c, part, send, keep, own, copy):
    me, right, opposite, left = neighbours()
    half = send.shape[3]
    sums = part(2, opposite)
    send[0, c] = sums[:, :half].astype(jnp.bfloat16)
    send[1, c] = sums[:, half:].astype(jnp.bfloat16)
    copy(0, c).start()
    copy(1, c).start()
    sums = part(1, right)
    send[2, c] = sums[:, :half].astype(jnp.bfloat16)
    keep[1, c] = sums[:, half:]
    copy(2, c).start()
    sums = part(3, left)
    send[3, c] = sums[:, half:].astype(jnp.bfloat16)
    keep[0, c] = sums[:, :half]
    copy(3, c).start()
    own[c] = part(0, me)


def pass_on(c, send, recv, keep, copy):
    for side in (0, 1):
        copy(side, c).wait_recv()
        send[4 + side, c] = (keep[side, c] + recv[side, c].astype(jnp.float32)).astype(
            jnp.bfloat16
        )
        copy(4 + side, c).start()


def last_sum(c, recv, own, copy):
    for kind in (2, 3, 4, 5):
        copy(kind, c).wait_recv()
    half = recv.shape[3]
    first = own[c, :, :half] + recv[2, c].astype(jnp.float32) + recv[4, c].astype(jnp.float32)
    second = own[c, :, half:] + recv[3, c].astype(jnp.float32) + recv[5, c].astype(jnp.float32)
    return first, second


def each(start, stop, body):
    lax.fori_loop(start, stop, lambda c, _: (body(c), 0)[1], 0)


def all_sent(chunks, copy):
    def wait(c):
        for kind in range(6):
            copy(kind, c).wait_send()

    each(0, chunks, wait)


def piece_scratch(chunks, rows, half):
    return [
        pltpu.VMEM((6, chunks, rows, half), jnp.bfloat16),
        pltpu.VMEM((6, chunks, rows, half), jnp.bfloat16),
        pltpu.VMEM((2, chunks, rows, half), jnp.float32),
        pltpu.VMEM((chunks, rows, 2 * half), jnp.float32),
        pltpu.SemaphoreType.DMA((6, chunks)),
        pltpu.SemaphoreType.DMA((6, chunks)),
    ]


def project_kernel(
    act_ref, w_ref, out_ref, weights, weight_sem, send, recv, keep, own, send_sem, recv_sem
):
    me, right, opposite, left = neighbours()
    chunks, rows, wide = own.shape
    half = wide // 2

    def load(k, dest, c):
        column = pl.multiple_of(dest * (chunks * wide) + c * wide, 128)
        return pltpu.make_async_copy(
            w_ref.at[:, pl.ds(column, wide)], weights.at[k, c], weight_sem.at[k, c]
        )

    for c in range(chunks):
        for k, dest in ((2, opposite), (1, right), (3, left), (0, me)):
            load(k, dest, c).start()
    greet((left, right))

    def copy(kind, c):
        return piece(kind, c, send, recv, send_sem, recv_sem)

    def first(c):
        def part(k, dest):
            load(k, dest, c).wait()
            return jnp.dot(act_ref[...], weights[k, c], preferred_element_type=jnp.float32)

        first_pieces(c, part, send, keep, own, copy)

    def last(c):
        low, high = last_sum(c, recv, own, copy)
        column = pl.multiple_of(c * wide, 128)
        out_ref[:, pl.ds(column, half)] = low.astype(jnp.bfloat16)
        out_ref[:, pl.ds(pl.multiple_of(column + half, 128), half)] = high.astype(jnp.bfloat16)

    each(0, chunks, first)
    each(0, chunks, lambda c: pass_on(c, send, recv, keep, copy))
    each(0, chunks, last)
    all_sent(chunks, copy)


def project(activated, weight):
    rows, depth = activated.shape
    width = weight.shape[1] // lax.axis_size("tensoror")
    wide = 256
    chunks = width // wide
    return pl.pallas_call(
        project_kernel,
        in_specs=[
            pl.BlockSpec(memory_space=pltpu.VMEM),
            pl.BlockSpec(memory_space=pl.ANY),
        ],
        out_specs=pl.BlockSpec(memory_space=pltpu.VMEM),
        out_shape=jax.ShapeDtypeStruct((rows, width), jnp.bfloat16),
        scratch_shapes=[
            pltpu.VMEM((4, chunks, depth, wide), jnp.bfloat16),
            pltpu.SemaphoreType.DMA((4, chunks)),
        ]
        + piece_scratch(chunks, rows, wide // 2),
        compiler_params=pltpu.CompilerParams(
            collective_id=1, has_side_effects=True, vmem_limit_bytes=VMEM
        ),
        cost_estimate=pl.CostEstimate(
            flops=8 * rows * depth * width, bytes_accessed=2 * weight.size, transcendentals=0
        ),
    )(activated, weight)


def heads_kernel(
    x_ref,
    square_ref,
    wkv_ref,
    wq_ref,
    kv_ref,
    q_ref,
    weights,
    squares,
    total,
    scale,
    weight_sem,
    square_send,
    square_recv,
    send,
    recv,
    keep,
    own,
    send_sem,
    recv_sem,
    *,
    width,
):
    me, right, opposite, left = neighbours()
    chunks, rows, wide = own.shape
    half = wide // 2
    extent = square_ref.shape[1]
    local = rows // extent
    kv_chunks = kv_ref.shape[1] // wide
    for c in range(chunks):
        source = wkv_ref if c < kv_chunks else wq_ref
        column = (c if c < kv_chunks else c - kv_chunks) * wide
        pltpu.make_async_copy(
            source.at[:, pl.ds(column, wide)], weights.at[c], weight_sem.at[c]
        ).start()
    greet((right, opposite, left))

    def square_copy(k, peer):
        return pltpu.make_async_remote_copy(
            src_ref=square_ref,
            dst_ref=squares.at[k],
            send_sem=square_send.at[k],
            recv_sem=square_recv.at[k],
            device_id={"tensoror": peer},
            device_id_type=MESH,
        )

    peers = ((1, right), (2, opposite), (3, left))
    for k, peer in peers:
        square_copy(k, peer).start()

    def copy(kind, c):
        return piece(kind, c, send, recv, send_sem, recv_sem)

    def first(c):
        pltpu.make_async_copy(
            wkv_ref.at[:, pl.ds(0, wide)], weights.at[c], weight_sem.at[c]
        ).wait()

        def part(k, dest):
            return jnp.dot(
                x_ref[pl.ds(pl.multiple_of(dest * rows, rows), rows), :],
                weights[c],
                preferred_element_type=jnp.float32,
            )

        first_pieces(c, part, send, keep, own, copy)

    each(0, chunks, first)
    for k, peer in peers:
        square_copy(k, peer).wait()
    total[...] = square_ref[...] + squares[1] + squares[2] + squares[3]
    diagonal = lax.broadcasted_iota(jnp.int32, (extent, extent), 0) == lax.broadcasted_iota(
        jnp.int32, (extent, extent), 1
    )
    for b in range(local):
        row = jnp.broadcast_to(total[pl.ds(me * local + b, 1), :], (extent, extent))
        column = jnp.sum(jnp.where(diagonal, row, 0.0), axis=1, keepdims=True)
        scale[pl.ds(b * extent, extent), :] = lax.rsqrt(column / width + epsilon)
    each(0, chunks, lambda c: pass_on(c, send, recv, keep, copy))

    def last(c, out_ref, base):
        low, high = last_sum(c, recv, own, copy)
        column = pl.multiple_of((c - base) * wide, 128)
        out_ref[:, pl.ds(column, half)] = (low * scale[...]).astype(jnp.bfloat16)
        out_ref[:, pl.ds(pl.multiple_of(column + half, 128), half)] = (
            high * scale[...]
        ).astype(jnp.bfloat16)

    each(0, kv_chunks, lambda c: last(c, kv_ref, 0))
    each(kv_chunks, chunks, lambda c: last(c, q_ref, kv_chunks))
    all_sent(chunks, copy)


def heads(mixed, squares, kv_weight, q_weight, full_width):
    count = lax.axis_size("tensoror")
    total, width = mixed.shape
    rows = total // count
    kv_cols = kv_weight.shape[1]
    q_cols = q_weight.shape[1]
    wide = 512
    chunks = (kv_cols + q_cols) // wide
    return pl.pallas_call(
        functools.partial(heads_kernel, width=full_width),
        in_specs=[
            pl.BlockSpec(memory_space=pltpu.VMEM),
            pl.BlockSpec(memory_space=pltpu.VMEM),
            pl.BlockSpec(memory_space=pl.ANY),
            pl.BlockSpec(memory_space=pl.ANY),
        ],
        out_specs=[pl.BlockSpec(memory_space=pltpu.VMEM)] * 2,
        out_shape=[
            jax.ShapeDtypeStruct((rows, kv_cols), jnp.bfloat16),
            jax.ShapeDtypeStruct((rows, q_cols), jnp.bfloat16),
        ],
        scratch_shapes=[
            pltpu.VMEM((chunks, width, wide), jnp.bfloat16),
            pltpu.VMEM((count,) + squares.shape, jnp.float32),
            pltpu.VMEM(squares.shape, jnp.float32),
            pltpu.VMEM((rows, 1), jnp.float32),
            pltpu.SemaphoreType.DMA((chunks,)),
            pltpu.SemaphoreType.DMA((count,)),
            pltpu.SemaphoreType.DMA((count,)),
        ]
        + piece_scratch(chunks, rows, wide // 2),
        compiler_params=pltpu.CompilerParams(
            collective_id=2, has_side_effects=True, vmem_limit_bytes=VMEM
        ),
        cost_estimate=pl.CostEstimate(
            flops=2 * total * width * (kv_cols + q_cols),
            bytes_accessed=2 * width * (kv_cols + q_cols),
            transcendentals=0,
        ),
    )(mixed, squares, kv_weight, q_weight)


def exchange_kernel(text_ref, after_ref, out_ref, buffer, send_sem, recv_sem, own_sem):
    count = lax.axis_size("tensoror")
    me = lax.axis_index("tensoror")
    local = text_ref.shape[0]
    depth = out_ref.shape[2]
    barrier = pltpu.get_barrier_semaphore()
    for k in range(1, count):
        pl.semaphore_signal(
            barrier,
            inc=1,
            device_id={"tensoror": lax.rem(me + k, count)},
            device_id_type=MESH,
        )
    pl.semaphore_wait(barrier, count - 1)
    copies = []
    for k in (2, 1, 3):
        peer = lax.rem(me + k, count)
        copies.append(
            pltpu.make_async_remote_copy(
                src_ref=text_ref.at[:, :, pl.ds(pl.multiple_of(peer * depth, 128), depth)],
                dst_ref=out_ref.at[pl.ds(me * local, local)],
                send_sem=send_sem.at[k],
                recv_sem=recv_sem.at[k],
                device_id={"tensoror": peer},
                device_id_type=MESH,
            )
        )
    for copy in copies:
        copy.start()
    own = pltpu.make_async_copy(
        text_ref.at[:, :, pl.ds(pl.multiple_of(me * depth, 128), depth)], buffer, own_sem.at[0]
    )
    own.start()
    own.wait()
    back = pltpu.make_async_copy(buffer, out_ref.at[pl.ds(me * local, local)], own_sem.at[1])
    back.start()
    back.wait()
    for copy in copies:
        copy.wait()


def exchange(text, after):
    count = lax.axis_size("tensoror")
    local, rows, width = text.shape
    depth = width // count
    return pl.pallas_call(
        exchange_kernel,
        in_specs=[pl.BlockSpec(memory_space=pl.ANY)] * 2,
        out_specs=pl.BlockSpec(memory_space=pl.ANY),
        out_shape=jax.ShapeDtypeStruct((local * count, rows, depth), text.dtype),
        scratch_shapes=[
            pltpu.VMEM((local, rows, depth), text.dtype),
            pltpu.SemaphoreType.DMA((4,)),
            pltpu.SemaphoreType.DMA((4,)),
            pltpu.SemaphoreType.DMA((2,)),
        ],
        compiler_params=pltpu.CompilerParams(
            collective_id=0, has_side_effects=True, vmem_limit_bytes=VMEM
        ),
        cost_estimate=pl.CostEstimate(
            flops=30_000_000_000, bytes_accessed=text.size * 4, transcendentals=0
        ),
    )(text, after)


def mix_kernel(
    start_ref, count_ref, visual_ref, text_ref, gain_ref, out_ref, square_ref, *, sequences
):
    step = pl.program_id(0)
    rows = text_ref.shape[1]
    width = text_ref.shape[2]
    group = lax.axis_index("group")
    place = lax.axis_index("seq")
    index = group * sequences + step
    start = start_ref[index]
    slots = TILE * count_ref[index]
    visual = visual_ref[...].reshape(-1, width)
    total = visual.shape[0]
    shift = place * rows - start
    slot = shift + lax.broadcasted_iota(jnp.int32, (rows, total), 0)
    column = lax.broadcasted_iota(jnp.int32, (rows, total), 1)
    pick = ((slot == column) & (column < slots)).astype(jnp.float32).astype(jnp.bfloat16)
    placed = jnp.dot(pick, visual, preferred_element_type=jnp.float32)
    own = shift + lax.broadcasted_iota(jnp.int32, (rows, width), 0)
    inside = (own >= 0) & (own < slots)
    mixed = jnp.where(inside, placed, text_ref[0].astype(jnp.float32))
    summed = lax.dot_general(
        jnp.ones((8, width), jnp.float32),
        mixed * mixed,
        (((1,), (1,)), ((), ())),
        precision=lax.Precision.HIGHEST,
        preferred_element_type=jnp.float32,
    )
    square_ref[pl.ds(step, 1), :] = summed[0:1]
    out_ref[...] = (mixed * gain_ref[...]).astype(jnp.bfloat16)


def mix(starts, counts, visual, text, gain):
    devices, sequences, part, width = visual.shape
    rows = text.shape[1]
    return pl.pallas_call(
        functools.partial(mix_kernel, sequences=sequences),
        grid_spec=pltpu.PrefetchScalarGridSpec(
            num_scalar_prefetch=2,
            grid=(sequences,),
            in_specs=[
                pl.BlockSpec((devices, 1, part, width), lambda j, *_: (0, j, 0, 0)),
                pl.BlockSpec((1, rows, width), lambda j, *_: (j, 0, 0)),
                pl.BlockSpec((1, width), lambda j, *_: (0, lax.axis_index("tensoror"))),
            ],
            out_specs=[
                pl.BlockSpec((rows, width), lambda j, *_: (j, 0)),
                pl.BlockSpec((sequences, rows), lambda j, *_: (0, 0)),
            ],
        ),
        out_shape=[
            jax.ShapeDtypeStruct((sequences * rows, width), jnp.bfloat16),
            jax.ShapeDtypeStruct((sequences, rows), jnp.float32),
        ],
        compiler_params=pltpu.CompilerParams(vmem_limit_bytes=VMEM),
        cost_estimate=pl.CostEstimate(
            flops=2 * devices * part * rows * width * sequences,
            bytes_accessed=2 * (visual.size + 2 * text.size),
            transcendentals=0,
        ),
    )(starts, counts, visual, text, gain)


def attend_kernel(q_ref, k_ref, v_ref, out_ref, stacked, top, low, total):
    rows = q_ref.shape[1]
    chunk = 512
    blocks = chunk // rows
    place = lax.axis_index("seq")
    factor = math.log2(math.e) / math.sqrt(HEAD_SIZE)
    for j in range(GROUP_HEADS):
        stacked[j * rows : (j + 1) * rows, :] = q_ref[0, :, j * HEAD_SIZE : (j + 1) * HEAD_SIZE]
    top[...] = jnp.full_like(top, masked_score)
    low[...] = jnp.zeros_like(low)
    total[...] = jnp.zeros_like(total)

    def absorb(c, masked):
        keys = k_ref[pl.ds(c * blocks, blocks)].reshape(chunk, HEAD_SIZE)
        values = v_ref[pl.ds(c * blocks, blocks)].reshape(chunk, HEAD_SIZE)
        scores = lax.dot_general(
            stacked[...], keys, (((1,), (1,)), ((), ())), preferred_element_type=jnp.float32
        )
        if masked:
            row = lax.rem(lax.broadcasted_iota(jnp.int32, scores.shape, 0), rows) + place * rows
            column = lax.broadcasted_iota(jnp.int32, scores.shape, 1) + c * chunk
            scores = jnp.where(column <= row, scores, masked_score)
        old = top[...]
        new = jnp.maximum(old, jnp.max(scores, axis=1, keepdims=True))
        expo = jnp.exp2((scores - new) * factor)
        keep = jnp.exp2((old - new) * factor)
        low[...] = low[...] * keep + jnp.sum(expo, axis=1, keepdims=True)
        total[...] = total[...] * keep + jnp.dot(
            expo.astype(jnp.bfloat16), values, preferred_element_type=jnp.float32
        )
        top[...] = new

    last = lax.div(place, blocks)
    lax.fori_loop(0, last, lambda c, _: (absorb(c, False), 0)[1], 0)
    absorb(last, True)
    result = total[...] / low[...]
    for j in range(GROUP_HEADS):
        out_ref[0, :, j * HEAD_SIZE : (j + 1) * HEAD_SIZE] = result[
            j * rows : (j + 1) * rows
        ].astype(jnp.bfloat16)


def attend(queries, keyvalues):
    local, rows, q_cols = queries.shape
    devices = keyvalues.shape[0]
    wide = GROUP_HEADS * HEAD_SIZE
    heads = KEY_VALUE_HEADS
    stack = GROUP_HEADS * rows
    return pl.pallas_call(
        attend_kernel,
        grid=(local, heads),
        in_specs=[
            pl.BlockSpec((1, rows, wide), lambda b, h: (b, 0, h)),
            pl.BlockSpec((devices, 1, rows, HEAD_SIZE), lambda b, h: (0, b, 0, h)),
            pl.BlockSpec((devices, 1, rows, HEAD_SIZE), lambda b, h: (0, b, 0, h + heads)),
        ],
        out_specs=pl.BlockSpec((1, rows, wide), lambda b, h: (b, 0, h)),
        out_shape=jax.ShapeDtypeStruct((local, rows, q_cols), jnp.bfloat16),
        scratch_shapes=[
            pltpu.VMEM((stack, HEAD_SIZE), jnp.bfloat16),
            pltpu.VMEM((stack, 1), jnp.float32),
            pltpu.VMEM((stack, 1), jnp.float32),
            pltpu.VMEM((stack, HEAD_SIZE), jnp.float32),
        ],
        compiler_params=pltpu.CompilerParams(vmem_limit_bytes=VMEM),
        cost_estimate=pl.CostEstimate(
            flops=4 * local * rows * q_cols * rows * devices,
            bytes_accessed=2 * keyvalues.size,
            transcendentals=0,
        ),
    )(queries, keyvalues, keyvalues)


def shards(
    visual_hidden,
    projector_weight,
    text_embeddings,
    tile_counts,
    image_start,
    norm_gain,
    query_weight,
    keyvalue_weight,
):
    sequence_local, extent_rows, width = text_embeddings.shape
    sequences, slot_rows, depth = visual_hidden.shape
    activated = jax.nn.gelu(visual_hidden.astype(jnp.float32), approximate=False).astype(
        jnp.bfloat16
    )
    visual = project(activated.reshape(sequences * slot_rows, depth), projector_weight)
    spread = lax.all_gather(visual, "seq", axis=0, tiled=False)
    spread = spread.reshape(-1, sequences, slot_rows, depth)
    text = exchange(text_embeddings, visual)
    mixed, squares = mix(image_start, tile_counts, spread, text, norm_gain.reshape(1, width))
    keyvalues, queries = heads(mixed, squares, keyvalue_weight, query_weight, width)
    gathered = lax.all_gather(
        keyvalues.reshape(sequence_local, extent_rows, -1), "seq", axis=0, tiled=False
    )
    return attend(queries.reshape(sequence_local, extent_rows, -1), gathered)


def solution(mesh):
    in_specs = (
        P("group", "seq", "tensoror"),
        P("tensoror", None),
        P(("group", "tensoror"), "seq", None),
        P(),
        P(),
        P(),
        P("tensoror", None),
        P("tensoror", None),
    )
    out_specs = P(("group", "tensoror"), "seq", None)
    return jax.shard_map(shards, mesh=mesh, in_specs=in_specs, out_specs=out_specs, check_vma=False)
```

time: 555 us -> 304 us (0.55); the launches traced: 545 us -> 302 us
  Pallas kernels: 0 us -> 201 us
  waiting for transfers between devices: 275 us -> 83.6 us
  matrix products: 77.5 us -> 0 us
  local copies, waits for them, and re-layouts: 73.9 us -> 0 us
  other arithmetic: 56.2 us -> 4.55 us
  blocking collectives: 34.2 us -> 0 us
  starting transfers between devices: 14.7 us -> 0.04 us
    pallas_call x0 -> x5, Pallas kernels: none -> 201 us  [the longest x1 68.2 us: heads(): pl.pallas_call(functools.partial(heads_kernel, width=full_width), in_spec...]
    reduce_scatter x2 -> x0, waiting for transfers between devices: 191 us -> none  [the longest x1 135 us: shards(): lax.psum_scatter(jnp.concatenate([jnp.dot(scattered, query_weight, prefer...]
    dot_general x11 -> x0, matrix products: 77.5 us -> none  [the longest x4 30.7 us: absorb_block(): jnp.einsum('sqkgd,srkd->sqkgr', query_rows, keys, preferred_element_type=...]
    all_gather x1 -> x2, waiting for transfers between devices: 45.5 us -> 83.5 us  [the longest x1 52.7 us: shards(): lax.all_gather(keyvalues.reshape(sequence_local, extent_rows, -1), 'seq',...]
    all_to_all x2 -> x0, waiting for transfers between devices: 37.9 us -> none  [the longest x1 30.3 us: shards(): lax.all_to_all(sent, 'seq', split_axis=1, concat_axis=1, tiled=True)]
    all_to_all x1 -> x0, blocking collectives: 34.2 us -> none  [shards(): lax.all_to_all(flat, 'tensoror', split_axis=1, concat_axis=0, tiled=True)]
    reduce_sum x5 -> x0, other arithmetic: 30.5 us -> none  [the longest x4 26.7 us: absorb_block(): denominator = denominator * rescale + jnp.sum(expo, axis=-1)]
    gather x4 -> x0, local copies, waits for them, and re-layouts: 24.5 us -> none  [the longest x1 10.3 us: shards(): sent = jnp.take_along_axis(held, wanted[:, :, None], axis=1)]
  transfers between devices with their start and end apart: 5 -> 2, of which waited for: 5 -> 2; matrix products, arithmetic and copies ran while one was open for 1% -> 0% of each run, Pallas kernels for 0% -> 11%
where the time goes in v1:
time: 304 us; the launch traced here: 302 us
  Pallas kernels  201 us (66%)
  waiting for transfers between devices  83.6 us (28%)
  between operations  13.4 us (4%)
  other arithmetic  4.55 us (1%)
    pallas_call x1, Pallas kernels, heads(): pl.pallas_call(functools.partial(heads_kernel, width=full_width), in_spec...  68.2 us
    pallas_call x1, Pallas kernels, attend(): pl.pallas_call(attend_kernel, grid=(local, heads), in_specs=[pl.BlockSpec...  59.5 us
    all_gather x1, waiting for transfers between devices, shards(): lax.all_gather(keyvalues.reshape(sequence_local, extent_rows, -1), 'seq',...  52.7 us
    pallas_call x1, Pallas kernels, exchange(): pl.pallas_call(exchange_kernel, in_specs=[pl.BlockSpec(memory_space=pl.AN...  32.2 us
    all_gather x1, waiting for transfers between devices, shards(): spread = lax.all_gather(visual, 'seq', axis=0, tiled=False)  30.9 us
    pallas_call x1, Pallas kernels, project(): pl.pallas_call(project_kernel, in_specs=[pl.BlockSpec(memory_space=pltpu....  28.2 us
    pallas_call x1, Pallas kernels, mix(): pl.pallas_call(functools.partial(mix_kernel, sequences=sequences), grid_s...  12.4 us
  transfers between devices with their start and end apart: 2, of which 2 were waited for; matrix products, arithmetic and copies ran while one was open for 0% of the time, Pallas kernels for 11%

profile of v1, /device:TPU:57, one launch (start us, length us, event | category | flops | bytes accessed | tf_op | source)
XLA Modules:
  0.0 302.1 jit_solution(4626831963287454638)
XLA Ops:
  6.5 0.0 all-gather.6.cloned.1.call-start
  6.5 4.5 %fusion.1 = bf16[8,32,1280]{2,1,0:T(8,128)(2,1)} fusion(bf16[8,32,1280]{2,1,0:T(8,128)(2,1)} %param.8), kind=kLoop, calls=%fused_computation.4 | loop fusion | flops 21626880 | bytes 1310720 | tf_op jit(solution)/shard_map/convert_element_type | solution.py:529
  11.1 28.2 %shard_map.82.after_ref = bf16[256,1280]{1,0:T(8,128)(2,1)} custom-call(bf16[256,1280]{1,0:T(8,128)(2,1)} %bitcast.6, bf16[1280,5120]{1,0:T(8,128)(2,1)} %w_ref.1), custom_call_target="tpu_custom_call" | custom-call | flops 3355443200 | bytes 13107200 | tf_op jit(solution)/shard_map/pallas_call | solution.py:158
  39.3 0.0 all-gather.6.cloned.1.call-update
  39.4 0.0 all-gather.4.cloned.1.call-start
  39.4 32.2 %shard_map.83.text_ref = bf16[8,128,1280]{2,1,0:T(8,128)(2,1)} custom-call(bf16[2,128,5120]{2,1,0:T(8,128)(2,1)} %text_ref.1, bf16[256,1280]{1,0:T(8,128)(2,1)} %shard_map.82.after_ref), custom_call_target="tpu_custom_call" | custom-call | flops 30000001024 | bytes 5242880 | tf_op jit(solution)/shard_map/pallas_call | solution.py:361
  71.7 30.9 %all-gather.6.cloned.1.call-done = bf16[4096,1280]{1,0:T(8,128)(2,1)} async-done(((bf16[256,1280]{1,0:T(8,128)(2,1)}), bf16[4096,1280]{1,0:T(8,128)(2,1)}) %all-gather.6.cloned.1.call-update) | async-done | bytes 10485776 | tf_op jit(solution)/shard_map/all_gather | solution.py:533
  102.5 12.4 %shard_map.84 = (bf16[1024,1280]{1,0:T(8,128)(2,1)}, f32[8,128]{1,0:T(8,128)}) custom-call(s32[16]{0:T(128)} %start_ref.1, s32[16]{0:T(128)} %count_ref.1, bf16[16,8,32,1280]{3,2,1,0:T(8,128)(2,1)} %bitcast.5, bf16[8,128,1280]{2,1,0:T(8,128)(2,1)} %shard_map.83.text_ref, f32[1,5120]{1,0:T(1,128)} %bitcast.8), custom_call_target="tpu_custom_call" | custom-call | flops 1342177280 | bytes 15728640 | tf_op jit(solution)/shard_map/pallas_call | solution.py:416
  114.9 68.2 %shard_map.85 = (bf16[256,1024]{1,0:T(8,128)(2,1)}, bf16[256,2560]{1,0:T(8,128)(2,1)}) custom-call(bf16[1024,1280]{1,0:T(8,128)(2,1)} %get-tuple-element.9.x_ref, f32[8,128]{1,0:T(8,128)} %get-tuple-element.10.square_ref, bf16[1280,1024]{1,0:T(8,128)(2,1)} %wkv_ref.1, bf16[1280,2560]{1,0:T(8,128)(2,1)} %wq_ref.1), custom_call_target="tpu_custom_call" | custom-call | flops 9395240960 | bytes 9175040 | tf_op jit(solution)/shard_map/pallas_call | solution.py:282
  183.1 0.0 all-gather.4.cloned.1.call-update
  183.1 52.7 %all-gather.4.cloned.1.call-done.k_ref.v_ref = bf16[16,2,128,1024]{3,2,1,0:T(8,128)(2,1)} async-done(((bf16[1,2,128,1024]{3,2,1,0:T(8,128)(2,1)}), bf16[16,2,128,1024]{3,2,1,0:T(8,128)(2,1)}) %all-gather.4.cloned.1.call-update) | async-done | bytes 8388624 | tf_op jit(solution)/shard_map/all_gather | solution.py:538
  235.8 59.5 %shard_map.86 = bf16[2,128,2560]{2,1,0:T(8,128)(2,1)} custom-call(bf16[2,128,2560]{2,1,0:T(8,128)(2,1)} %bitcast.9, bf16[16,2,128,1024]{3,2,1,0:T(8,128)(2,1)} %all-gather.4.cloned.1.call-done.k_ref.v_ref, bf16[16,2,128,1024]{3,2,1,0:T(8,128)(2,1)} %all-gather.4.cloned.1.call-done.k_ref.v_ref), custom_call_target="tpu_custom_call" | custom-call | flops 5368709120 | bytes 8388608 | tf_op jit(solution)/shard_map/pallas_call | solution.py:492
Async XLA Ops:
  6.5 96.0 %all-gather.6.cloned.1.call-start = ((), (), s32[]{:S(2)}) async-start(), calls=%async_computation.1 | async-start | bytes 11141120 | tf_op jit(solution)/shard_map/all_gather | solution.py:533
  39.4 196.4 %all-gather.4.cloned.1.call-start = ((), (), s32[]{:S(2)}) async-start(), calls=%async_computation | async-start | bytes 8912896 | tf_op jit(solution)/shard_map/all_gather | solution.py:538
Sparse Core Ops, SparseCore 0:
  39.5 62.9 all-gather.5
  183.2 52.4 all-gather.3

commit v2 on v1

--- a/solution.py
+++ b/solution.py
@@ -30,7 +30,7 @@
     barrier = pltpu.get_barrier_semaphore()
     for peer in peers:
         pl.semaphore_signal(
-            barrier, inc=1, device_id={"tensoror": peer}, device_id_type=MESH
+            barrier, inc=1, device_id=peer, device_id_type=MESH
         )
     pl.semaphore_wait(barrier, len(peers))
 
@@ -126,7 +126,7 @@
     for c in range(chunks):
         for k, dest in ((2, opposite), (1, right), (3, left), (0, me)):
             load(k, dest, c).start()
-    greet((left, right))
+    greet([{"tensoror": peer} for peer in (left, right)])
 
     def copy(kind, c):
         return piece(kind, c, send, recv, send_sem, recv_sem)
@@ -212,7 +212,7 @@
         pltpu.make_async_copy(
             source.at[:, pl.ds(column, wide)], weights.at[c], weight_sem.at[c]
         ).start()
-    greet((right, opposite, left))
+    greet([{"tensoror": peer} for peer in (right, opposite, left)])
 
     def square_copy(k, peer):
         return pltpu.make_async_remote_copy(
@@ -313,205 +313,352 @@
     )(mixed, squares, kv_weight, q_weight)
 
 
-def exchange_kernel(text_ref, after_ref, out_ref, buffer, send_sem, recv_sem, own_sem):
-    count = lax.axis_size("tensoror")
-    me = lax.axis_index("tensoror")
+OWN, NEXT, PREV, ACROSS, PARTNER = (0, 0, 0), (1, 0, 0), (3, 0, 0), (0, 1, 0), (0, 0, 1)
+FAR = (2, 0, 0)
+KINDS = {
+    "next": (OWN, PREV, None),
+    "prev": (OWN, NEXT, None),
+    "across": (OWN, ACROSS, None),
+    "partner": (OWN, PARTNER, None),
+    "far0": (NEXT, PREV, 0),
+    "far1": (PREV, NEXT, 1),
+    "next_across": (ACROSS, PREV, None),
+    "prev_across": (ACROSS, NEXT, None),
+    "far_across0": (FAR, ACROSS, 0),
+    "far_across1": (FAR, ACROSS, 1),
+}
+GOT = {
+    "next": NEXT,
+    "prev": PREV,
+    "across": ACROSS,
+    "partner": PARTNER,
+    "far0": FAR,
+    "far1": FAR,
+    "next_across": (1, 1, 0),
+    "prev_across": (3, 1, 0),
+    "far_across0": (2, 1, 0),
+    "far_across1": (2, 1, 0),
+}
+for name in list(GOT):
+    if name != "partner":
+        KINDS["twin_" + name] = (GOT[name], PARTNER, KINDS[name][2])
+        GOT["twin_" + name] = GOT[name][:2] + (1,)
+ORDER = {name: k for k, name in enumerate(KINDS)}
+
+
+def seq_at(offset):
+    place = lax.axis_index("seq")
+    y = lax.rem(lax.div(place, 4) + offset[0], 4)
+    z = lax.rem(lax.div(place, 2) + offset[1], 2)
+    core = lax.rem(place + offset[2], 2)
+    return y * 4 + z * 2 + core
+
+
+class Gather:
+    def __init__(self, own_ref, blocks, send_sem, recv_sem):
+        self.refs = own_ref, blocks, send_sem, recv_sem
+
+    def copy(self, name, arrival):
+        own_ref, blocks, send_sem, recv_sem = self.refs
+        block, target, half = KINDS[name]
+        rows = blocks.shape[1]
+        cut = pl.ds(0, rows) if half is None else pl.ds(half * (rows // 2), rows // 2)
+        where = blocks.at[seq_at(GOT[name] if arrival else block), cut]
+        source = own_ref if block == OWN and not arrival else where
+        k = ORDER[name]
+        return pltpu.make_async_remote_copy(
+            src_ref=source,
+            dst_ref=where,
+            send_sem=send_sem.at[k],
+            recv_sem=recv_sem.at[k],
+            device_id={"seq": seq_at(target)},
+            device_id_type=MESH,
+        )
+
+    def start(self, *names):
+        for name in names:
+            self.copy(name, False).start()
+
+    def arrived(self, *names):
+        for name in names:
+            self.copy(name, True).wait_recv()
+
+    def finish(self):
+        for name in KINDS:
+            self.copy(name, False).wait_send()
+
+
+def seq_peers():
+    return [{"seq": seq_at(offset)} for offset in (NEXT, PREV, ACROSS, PARTNER)]
+
+
+GATHER_SEMAPHORES = [
+    pltpu.SemaphoreType.DMA((len(KINDS),)),
+    pltpu.SemaphoreType.DMA((len(KINDS),)),
+]
+
+
+def mix_kernel(
+    start_ref,
+    count_ref,
+    visual_ref,
+    text_ref,
+    gain_ref,
+    out_ref,
+    square_ref,
+    blocks,
+    text,
+    text_send,
+    text_recv,
+    own_sem,
+    send_sem,
+    recv_sem,
+):
+    me, right, opposite, left = neighbours()
+    group = lax.axis_index("group")
+    place = lax.axis_index("seq")
     local = text_ref.shape[0]
-    depth = out_ref.shape[2]
-    barrier = pltpu.get_barrier_semaphore()
-    for k in range(1, count):
-        pl.semaphore_signal(
-            barrier,
-            inc=1,
-            device_id={"tensoror": lax.rem(me + k, count)},
-            device_id_type=MESH,
-        )
-    pl.semaphore_wait(barrier, count - 1)
-    copies = []
-    for k in (2, 1, 3):
-        peer = lax.rem(me + k, count)
-        copies.append(
+    sequences, rows, width = text.shape
+    part = blocks.shape[1] // sequences
+    gather = Gather(visual_ref, blocks, send_sem, recv_sem)
+
+    def columns(peer):
+        return text_ref.at[:, :, pl.ds(pl.multiple_of(peer * width, 128), width)]
+
+    own_text = pltpu.make_async_copy(columns(me), text.at[pl.ds(me * local, local)], own_sem)
+    own_text.start()
+    greet([{"tensoror": peer} for peer in (right, opposite, left)] + seq_peers())
+    gather.start("next", "prev", "across", "partner")
+    exchanges = []
+    for k, peer in ((2, opposite), (1, right), (3, left)):
+        exchanges.append(
             pltpu.make_async_remote_copy(
-                src_ref=text_ref.at[:, :, pl.ds(pl.multiple_of(peer * depth, 128), depth)],
-                dst_ref=out_ref.at[pl.ds(me * local, local)],
-                send_sem=send_sem.at[k],
-                recv_sem=recv_sem.at[k],
+                src_ref=columns(peer),
+                dst_ref=text.at[pl.ds(me * local, local)],
+                send_sem=text_send.at[k],
+                recv_sem=text_recv.at[k],
                 device_id={"tensoror": peer},
                 device_id_type=MESH,
             )
         )
-    for copy in copies:
-        copy.start()
-    own = pltpu.make_async_copy(
-        text_ref.at[:, :, pl.ds(pl.multiple_of(me * depth, 128), depth)], buffer, own_sem.at[0]
+    for exchange in exchanges:
+        exchange.start()
+    blocks[place] = visual_ref[...]
+    gather.arrived("next")
+    gather.start("far0", "twin_next")
+    gather.arrived("prev")
+    gather.start("far1", "twin_prev")
+    gather.arrived("across")
+    gather.start("next_across", "prev_across", "twin_across")
+    gather.arrived("far0")
+    gather.start("far_across0", "twin_far0")
+    gather.arrived("far1")
+    gather.start("far_across1", "twin_far1")
+    gather.arrived("next_across")
+    gather.start("twin_next_across")
+    gather.arrived("prev_across")
+    gather.start("twin_prev_across")
+    gather.arrived("far_across0")
+    gather.start("twin_far_across0")
+    gather.arrived("far_across1")
+    gather.start("twin_far_across1")
+    gather.arrived("partner", *[name for name in KINDS if name.startswith("twin_")])
+    own_text.wait()
+    for exchange in exchanges:
+        exchange.wait()
+    diagonal = lax.broadcasted_iota(jnp.int32, (rows, rows), 0) == lax.broadcasted_iota(
+        jnp.int32, (rows, rows), 1
     )
-    own.start()
-    own.wait()
-    back = pltpu.make_async_copy(buffer, out_ref.at[pl.ds(me * local, local)], own_sem.at[1])
-    back.start()
-    back.wait()
-    for copy in copies:
-        copy.wait()
-
-
-def exchange(text, after):
+
+    def one(i):
+        start = start_ref[group * sequences + i]
+        slots = TILE * count_ref[group * sequences + i]
+        visual = blocks[:, pl.ds(pl.multiple_of(i * part, part), part), :].reshape(-1, width)
+        total = visual.shape[0]
+        shift = place * rows - start
+        slot = shift + lax.broadcasted_iota(jnp.int32, (rows, total), 0)
+        column = lax.broadcasted_iota(jnp.int32, (rows, total), 1)
+        pick = jnp.where((slot == column) & (column < slots), 1.0, 0.0).astype(jnp.bfloat16)
+        placed = jnp.dot(pick, visual, preferred_element_type=jnp.float32)
+        own = shift + lax.broadcasted_iota(jnp.int32, (rows, width), 0)
+        inside = (own >= 0) & (own < slots)
+        mixed = jnp.where(inside, placed, text[i].astype(jnp.float32))
+        squares = jnp.sum(mixed * mixed, axis=1, keepdims=True)
+        square_ref[pl.ds(i, 1), :] = jnp.sum(
+            jnp.where(diagonal, squares, 0.0), axis=0, keepdims=True
+        )
+        out_ref[pl.ds(pl.multiple_of(i * rows, rows), rows), :] = (mixed * gain_ref[...]).astype(
+            jnp.bfloat16
+        )
+
+    each(0, sequences, one)
+    gather.finish()
+
+
+def mix(starts, counts, visual, text, gain):
+    devices = lax.axis_size("seq")
     count = lax.axis_size("tensoror")
-    local, rows, width = text.shape
-    depth = width // count
+    local, rows, full = text.shape
+    width = full // count
+    sequences = local * count
+    smem = pl.BlockSpec(memory_space=pltpu.SMEM)
+    vmem = pl.BlockSpec(memory_space=pltpu.VMEM)
     return pl.pallas_call(
-        exchange_kernel,
-        in_specs=[pl.BlockSpec(memory_space=pl.ANY)] * 2,
-        out_specs=pl.BlockSpec(memory_space=pl.ANY),
-        out_shape=jax.ShapeDtypeStruct((local * count, rows, depth), text.dtype),
-        scratch_shapes=[
-            pltpu.VMEM((local, rows, depth), text.dtype),
-            pltpu.SemaphoreType.DMA((4,)),
-            pltpu.SemaphoreType.DMA((4,)),
-            pltpu.SemaphoreType.DMA((2,)),
-        ],
-        compiler_params=pltpu.CompilerParams(
-            collective_id=0, has_side_effects=True, vmem_limit_bytes=VMEM
-        ),
-        cost_estimate=pl.CostEstimate(
-            flops=30_000_000_000, bytes_accessed=text.size * 4, transcendentals=0
-        ),
-    )(text, after)
-
-
-def mix_kernel(
-    start_ref, count_ref, visual_ref, text_ref, gain_ref, out_ref, square_ref, *, sequences
-):
-    step = pl.program_id(0)
-    rows = text_ref.shape[1]
-    width = text_ref.shape[2]
-    group = lax.axis_index("group")
-    place = lax.axis_index("seq")
-    index = group * sequences + step
-    start = start_ref[index]
-    slots = TILE * count_ref[index]
-    visual = visual_ref[...].reshape(-1, width)
-    total = visual.shape[0]
-    shift = place * rows - start
-    slot = shift + lax.broadcasted_iota(jnp.int32, (rows, total), 0)
-    column = lax.broadcasted_iota(jnp.int32, (rows, total), 1)
-    pick = ((slot == column) & (column < slots)).astype(jnp.float32).astype(jnp.bfloat16)
-    placed = jnp.dot(pick, visual, preferred_element_type=jnp.float32)
-    own = shift + lax.broadcasted_iota(jnp.int32, (rows, width), 0)
-    inside = (own >= 0) & (own < slots)
-    mixed = jnp.where(inside, placed, text_ref[0].astype(jnp.float32))
-    summed = lax.dot_general(
-        jnp.ones((8, width), jnp.float32),
-        mixed * mixed,
-        (((1,), (1,)), ((), ())),
-        precision=lax.Precision.HIGHEST,
-        preferred_element_type=jnp.float32,
-    )
-    square_ref[pl.ds(step, 1), :] = summed[0:1]
-    out_ref[...] = (mixed * gain_ref[...]).astype(jnp.bfloat16)
-
-
-def mix(starts, counts, visual, text, gain):
-    devices, sequences, part, width = visual.shape
-    rows = text.shape[1]
-    return pl.pallas_call(
-        functools.partial(mix_kernel, sequences=sequences),
-        grid_spec=pltpu.PrefetchScalarGridSpec(
-            num_scalar_prefetch=2,
-            grid=(sequences,),
-            in_specs=[
-                pl.BlockSpec((devices, 1, part, width), lambda j, *_: (0, j, 0, 0)),
-                pl.BlockSpec((1, rows, width), lambda j, *_: (j, 0, 0)),
-                pl.BlockSpec((1, width), lambda j, *_: (0, lax.axis_index("tensoror"))),
-            ],
-            out_specs=[
-                pl.BlockSpec((rows, width), lambda j, *_: (j, 0)),
-                pl.BlockSpec((sequences, rows), lambda j, *_: (0, 0)),
-            ],
-        ),
+        mix_kernel,
+        in_specs=[smem, smem, vmem, pl.BlockSpec(memory_space=pl.ANY), vmem],
+        out_specs=[vmem, vmem],
         out_shape=[
             jax.ShapeDtypeStruct((sequences * rows, width), jnp.bfloat16),
             jax.ShapeDtypeStruct((sequences, rows), jnp.float32),
         ],
-        compiler_params=pltpu.CompilerParams(vmem_limit_bytes=VMEM),
-        cost_estimate=pl.CostEstimate(
-            flops=2 * devices * part * rows * width * sequences,
-            bytes_accessed=2 * (visual.size + 2 * text.size),
-            transcendentals=0,
+        scratch_shapes=[
+            pltpu.VMEM((devices,) + visual.shape, jnp.bfloat16),
+            pltpu.VMEM((sequences, rows, width), jnp.bfloat16),
+            pltpu.SemaphoreType.DMA((4,)),
+            pltpu.SemaphoreType.DMA((4,)),
+            pltpu.SemaphoreType.DMA,
+        ]
+        + GATHER_SEMAPHORES,
+        compiler_params=pltpu.CompilerParams(
+            collective_id=0, has_side_effects=True, vmem_limit_bytes=VMEM
         ),
     )(starts, counts, visual, text, gain)
 
 
-def attend_kernel(q_ref, k_ref, v_ref, out_ref, stacked, top, low, total):
-    rows = q_ref.shape[1]
-    chunk = 512
-    blocks = chunk // rows
+def attend_kernel(
+    q_ref, kv_ref, out_ref, blocks, queries, top, low, total, send_sem, recv_sem
+):
     place = lax.axis_index("seq")
+    rows = HEAD_SIZE
+    units = queries.shape[0]
     factor = math.log2(math.e) / math.sqrt(HEAD_SIZE)
-    for j in range(GROUP_HEADS):
-        stacked[j * rows : (j + 1) * rows, :] = q_ref[0, :, j * HEAD_SIZE : (j + 1) * HEAD_SIZE]
+    gather = Gather(kv_ref, blocks, send_sem, recv_sem)
+    greet(seq_peers())
+    gather.start("next", "prev", "across", "partner")
+    blocks[place] = kv_ref[...]
+    for u in range(units):
+        b, h = divmod(u, KEY_VALUE_HEADS)
+        for j in range(GROUP_HEADS):
+            column = (h * GROUP_HEADS + j) * HEAD_SIZE
+            queries[u, j * rows : (j + 1) * rows, :] = q_ref[
+                b * rows : (b + 1) * rows, column : column + HEAD_SIZE
+            ]
     top[...] = jnp.full_like(top, masked_score)
     low[...] = jnp.zeros_like(low)
     total[...] = jnp.zeros_like(total)
 
-    def absorb(c, masked):
-        keys = k_ref[pl.ds(c * blocks, blocks)].reshape(chunk, HEAD_SIZE)
-        values = v_ref[pl.ds(c * blocks, blocks)].reshape(chunk, HEAD_SIZE)
+    def absorb(u, chip, masked):
+        b = pl.ds(pl.multiple_of(lax.div(u, KEY_VALUE_HEADS) * rows, rows), rows)
+        h = lax.rem(u, KEY_VALUE_HEADS) * HEAD_SIZE
+        pair = pl.ds(2 * chip, 2)
+        keys = blocks[pair, b, pl.ds(pl.multiple_of(h, 128), HEAD_SIZE)]
+        values = blocks[
+            pair, b, pl.ds(pl.multiple_of(h + KEY_VALUE_HEADS * HEAD_SIZE, 128), HEAD_SIZE)
+        ]
         scores = lax.dot_general(
-            stacked[...], keys, (((1,), (1,)), ((), ())), preferred_element_type=jnp.float32
+            keys.reshape(2 * rows, HEAD_SIZE),
+            queries[u],
+            (((1,), (1,)), ((), ())),
+            preferred_element_type=jnp.float32,
         )
         if masked:
-            row = lax.rem(lax.broadcasted_iota(jnp.int32, scores.shape, 0), rows) + place * rows
-            column = lax.broadcasted_iota(jnp.int32, scores.shape, 1) + c * chunk
-            scores = jnp.where(column <= row, scores, masked_score)
-        old = top[...]
-        new = jnp.maximum(old, jnp.max(scores, axis=1, keepdims=True))
+            key = lax.broadcasted_iota(jnp.int32, scores.shape, 0)
+            query = (
+                lax.rem(lax.broadcasted_iota(jnp.int32, scores.shape, 1), rows)
+                + lax.rem(place, 2) * rows
+            )
+            scores = jnp.where(key <= query, scores, masked_score)
+        old = top[u]
+        new = jnp.maximum(old, jnp.max(scores, axis=0, keepdims=True))
         expo = jnp.exp2((scores - new) * factor)
         keep = jnp.exp2((old - new) * factor)
-        low[...] = low[...] * keep + jnp.sum(expo, axis=1, keepdims=True)
-        total[...] = total[...] * keep + jnp.dot(
-            expo.astype(jnp.bfloat16), values, preferred_element_type=jnp.float32
-        )
-        top[...] = new
-
-    last = lax.div(place, blocks)
-    lax.fori_loop(0, last, lambda c, _: (absorb(c, False), 0)[1], 0)
-    absorb(last, True)
-    result = total[...] / low[...]
-    for j in range(GROUP_HEADS):
-        out_ref[0, :, j * HEAD_SIZE : (j + 1) * HEAD_SIZE] = result[
-            j * rows : (j + 1) * rows
-        ].astype(jnp.bfloat16)
+        low[u] = low[u] * keep + jnp.sum(expo, axis=0, keepdims=True)
+        total[u] = total[u] * keep + lax.dot_general(
+            values.reshape(2 * rows, HEAD_SIZE),
+            expo.astype(jnp.bfloat16),
+            (((0,), (0,)), ((), ())),
+            preferred_element_type=jnp.float32,
+        )
+        top[u] = new
+
+    chip = lax.div(place, 2)
+
+    def absorb_all(offset):
+        other = lax.div(seq_at(offset), 2)
+
+        @pl.when(other < chip)
+        def _():
+            each(0, units, lambda u: absorb(u, other, False))
+
+    gather.arrived("partner")
+    each(0, units, lambda u: absorb(u, chip, True))
+    gather.arrived("next")
+    gather.start("far0", "twin_next")
+    gather.arrived("prev")
+    gather.start("far1", "twin_prev")
+    gather.arrived("across")
+    gather.start("next_across", "prev_across", "twin_across")
+    gather.arrived("twin_next")
+    absorb_all(NEXT)
+    gather.arrived("far0")
+    gather.start("far_across0", "twin_far0")
+    gather.arrived("far1")
+    gather.start("far_across1", "twin_far1")
+    gather.arrived("twin_prev")
+    absorb_all(PREV)
+    gather.arrived("twin_across")
+    absorb_all(ACROSS)
+    gather.arrived("twin_far0", "twin_far1")
+    absorb_all(FAR)
+    gather.arrived("next_across")
+    gather.start("twin_next_across")
+    gather.arrived("prev_across")
+    gather.start("twin_prev_across")
+    gather.arrived("far_across0")
+    gather.start("twin_far_across0")
+    gather.arrived("far_across1")
+    gather.start("twin_far_across1")
+    gather.arrived("twin_next_across")
+    absorb_all((1, 1, 0))
+    gather.arrived("twin_prev_across")
+    absorb_all((3, 1, 0))
+    gather.arrived("twin_far_across0", "twin_far_across1")
+    absorb_all((2, 1, 0))
+
+    for u in range(units):
+        b, h = divmod(u, KEY_VALUE_HEADS)
+        result = total[u] / low[u]
+        for j in range(GROUP_HEADS):
+            column = (h * GROUP_HEADS + j) * HEAD_SIZE
+            out_ref[b * rows : (b + 1) * rows, column : column + HEAD_SIZE] = jnp.transpose(
+                result[:, j * rows : (j + 1) * rows]
+            ).astype(jnp.bfloat16)
+    gather.finish()
 
 
 def attend(queries, keyvalues):
-    local, rows, q_cols = queries.shape
-    devices = keyvalues.shape[0]
-    wide = GROUP_HEADS * HEAD_SIZE
-    heads = KEY_VALUE_HEADS
-    stack = GROUP_HEADS * rows
+    devices = lax.axis_size("seq")
+    rows, q_cols = queries.shape
+    units = rows // HEAD_SIZE * KEY_VALUE_HEADS
+    stack = GROUP_HEADS * HEAD_SIZE
+    vmem = pl.BlockSpec(memory_space=pltpu.VMEM)
     return pl.pallas_call(
         attend_kernel,
-        grid=(local, heads),
-        in_specs=[
-            pl.BlockSpec((1, rows, wide), lambda b, h: (b, 0, h)),
-            pl.BlockSpec((devices, 1, rows, HEAD_SIZE), lambda b, h: (0, b, 0, h)),
-            pl.BlockSpec((devices, 1, rows, HEAD_SIZE), lambda b, h: (0, b, 0, h + heads)),
-        ],
-        out_specs=pl.BlockSpec((1, rows, wide), lambda b, h: (b, 0, h)),
-        out_shape=jax.ShapeDtypeStruct((local, rows, q_cols), jnp.bfloat16),
+        in_specs=[vmem, vmem],
+        out_specs=vmem,
+        out_shape=jax.ShapeDtypeStruct((rows, q_cols), jnp.bfloat16),
         scratch_shapes=[
-            pltpu.VMEM((stack, HEAD_SIZE), jnp.bfloat16),
-            pltpu.VMEM((stack, 1), jnp.float32),
-            pltpu.VMEM((stack, 1), jnp.float32),
-            pltpu.VMEM((stack, HEAD_SIZE), jnp.float32),
-        ],
-        compiler_params=pltpu.CompilerParams(vmem_limit_bytes=VMEM),
-        cost_estimate=pl.CostEstimate(
-            flops=4 * local * rows * q_cols * rows * devices,
-            bytes_accessed=2 * keyvalues.size,
-            transcendentals=0,
+            pltpu.VMEM((devices,) + keyvalues.shape, jnp.bfloat16),
+            pltpu.VMEM((units, stack, HEAD_SIZE), jnp.bfloat16),
+            pltpu.VMEM((units, 1, stack), jnp.float32),
+            pltpu.VMEM((units, 1, stack), jnp.float32),
+            pltpu.VMEM((units, HEAD_SIZE, stack), jnp.float32),
+        ]
+        + GATHER_SEMAPHORES,
+        compiler_params=pltpu.CompilerParams(
+            collective_id=3, has_side_effects=True, vmem_limit_bytes=VMEM
         ),
-    )(queries, keyvalues, keyvalues)
+    )(queries, keyvalues)
 
 
 def shards(
@@ -530,15 +677,10 @@
         jnp.bfloat16
     )
     visual = project(activated.reshape(sequences * slot_rows, depth), projector_weight)
-    spread = lax.all_gather(visual, "seq", axis=0, tiled=False)
-    spread = spread.reshape(-1, sequences, slot_rows, depth)
-    text = exchange(text_embeddings, visual)
-    mixed, squares = mix(image_start, tile_counts, spread, text, norm_gain.reshape(1, width))
+    gain = lax.dynamic_slice_in_dim(norm_gain, lax.axis_index("tensoror") * depth, depth)
+    mixed, squares = mix(image_start, tile_counts, visual, text_embeddings, gain.reshape(1, depth))
     keyvalues, queries = heads(mixed, squares, keyvalue_weight, query_weight, width)
-    gathered = lax.all_gather(
-        keyvalues.reshape(sequence_local, extent_rows, -1), "seq", axis=0, tiled=False
-    )
-    return attend(queries.reshape(sequence_local, extent_rows, -1), gathered)
+    return attend(queries, keyvalues).reshape(sequence_local, extent_rows, -1)
 
 
 def solution(mesh):

time: 304 us -> 209 us (0.69)
  waiting for transfers between devices: 83.6 us -> 0 us
  between operations: 13.4 us -> 0.03 us
  local copies, waits for them, and re-layouts: 0 us -> 3.83 us
    all_gather x2 -> x0, waiting for transfers between devices: 83.5 us -> none  [the longest x1 52.7 us: shards(): lax.all_gather(keyvalues.reshape(sequence_local, extent_rows, -1), 'seq',...]
    pallas_call x3 -> x2, Pallas kernels: 104 us -> 105 us  [the longest x1 55.7 us: attend(): pl.pallas_call(attend_kernel, in_specs=[vmem, vmem], out_specs=vmem, out_...]
  transfers between devices with their start and end apart: 2 -> 0, of which waited for: 2 -> 0; matrix products, arithmetic and copies ran while one was open for 0% -> 0% of each run, Pallas kernels for 11% -> 0%
where the time goes in v2:
time: 209 us
  Pallas kernels  200 us (96%)
  other arithmetic  4.55 us (2%)
  local copies, waits for them, and re-layouts  3.83 us (2%)
    pallas_call x1, Pallas kernels, heads(): pl.pallas_call(functools.partial(heads_kernel, width=full_width), in_spec...  66.5 us
    pallas_call x1, Pallas kernels, attend(): pl.pallas_call(attend_kernel, in_specs=[vmem, vmem], out_specs=vmem, out_...  55.7 us
    pallas_call x1, Pallas kernels, mix(): pl.pallas_call(mix_kernel, in_specs=[smem, smem, vmem, pl.BlockSpec(memor...  49.6 us
    pallas_call x1, Pallas kernels, project(): pl.pallas_call(project_kernel, in_specs=[pl.BlockSpec(memory_space=pltpu....  28.2 us
    convert_element_type x1, other arithmetic, shards(): jax.nn.gelu(visual_hidden.astype(jnp.float32), approximate=False)  4.55 us

profile of v2, /device:TPU:57, one launch (start us, length us, event | category | flops | bytes accessed | tf_op | source)
XLA Modules:
  0.0 208.5 jit_solution(7941638054646827942)
XLA Ops:
  0.0 0.8 dynamic_slice.3
  0.8 0.6 reshape.10.gain_ref
  1.4 4.5 %fusion.1 = bf16[8,32,1280]{2,1,0:T(8,128)(2,1)} fusion(bf16[8,32,1280]{2,1,0:T(8,128)(2,1)} %param.8), kind=kLoop, calls=%fused_computation.4 | loop fusion | flops 21626880 | bytes 1310720 | tf_op jit(solution)/shard_map/convert_element_type | solution.py:676
  5.9 28.2 %shard_map.82.visual_ref = bf16[256,1280]{1,0:T(8,128)(2,1)} custom-call(bf16[256,1280]{1,0:T(8,128)(2,1)} %bitcast.3, bf16[1280,5120]{1,0:T(8,128)(2,1)} %w_ref.1), custom_call_target="tpu_custom_call" | custom-call | flops 3355443200 | bytes 13107200 | tf_op jit(solution)/shard_map/pallas_call | solution.py:158
  34.2 49.6 %shard_map.83 = (bf16[1024,1280]{1,0:T(8,128)(2,1)}, f32[8,128]{1,0:T(8,128)}) custom-call(s32[16]{0:T(128)} %start_ref.1, s32[16]{0:T(128)} %count_ref.1, bf16[256,1280]{1,0:T(8,128)(2,1)} %shard_map.82.visual_ref, bf16[2,128,5120]{2,1,0:T(8,128)(2,1)} %text_ref.1, f32[1,1280]{1,0:T(1,128)} %reshape.10.gain_ref), custom_call_target="tpu_custom_call" | custom-call | tf_op jit(solution)/shard_map/pallas_call | solution.py:506
  83.8 66.5 %shard_map.84 = (bf16[256,1024]{1,0:T(8,128)(2,1)}, bf16[256,2560]{1,0:T(8,128)(2,1)}) custom-call(bf16[1024,1280]{1,0:T(8,128)(2,1)} %get-tuple-element.9.x_ref, f32[8,128]{1,0:T(8,128)} %get-tuple-element.10.square_ref, bf16[1280,1024]{1,0:T(8,128)(2,1)} %wkv_ref.1, bf16[1280,2560]{1,0:T(8,128)(2,1)} %wq_ref.1), custom_call_target="tpu_custom_call" | custom-call | flops 9395240960 | bytes 9175040 | tf_op jit(solution)/shard_map/pallas_call | solution.py:282
  150.3 55.7 %shard_map.85 = bf16[256,2560]{1,0:T(8,128)(2,1)} custom-call(bf16[256,2560]{1,0:T(8,128)(2,1)} %get-tuple-element.11.q_ref, bf16[256,1024]{1,0:T(8,128)(2,1)} %get-tuple-element.12.kv_ref), custom_call_target="tpu_custom_call" | custom-call | tf_op jit(solution)/shard_map/pallas_call | solution.py:645
  206.1 2.5 %copy.10 = bf16[2,128,2560]{2,1,0:T(8,128)(2,1)} copy(bf16[2,128,2560]{2,1,0:T(8,128)(2,1)} %bitcast.2) | data formatting | bytes 2621440

commit v3 on v2

v3 whole, which is shorter than its diff:
```python
import functools
import math

import jax
import jax.numpy as jnp
from jax import lax
from jax.experimental import pallas as pl
from jax.experimental.pallas import tpu as pltpu
from jax.sharding import PartitionSpec as P

QUERY_HEADS = 20
KEY_VALUE_HEADS = 4
HEAD_SIZE = 128
TILE = 256
GROUP_HEADS = QUERY_HEADS // KEY_VALUE_HEADS
MESH = pl.DeviceIdType.MESH

epsilon = 1e-06
masked_score = -1e30
VMEM = 60 * 1024 * 1024


def neighbours():
    count = lax.axis_size("tensoror")
    me = lax.axis_index("tensoror")
    return me, lax.rem(me + 1, count), lax.rem(me + 2, count), lax.rem(me + 3, count)


def greet(peers):
    barrier = pltpu.get_barrier_semaphore()
    for peer in peers:
        pl.semaphore_signal(
            barrier, inc=1, device_id=peer, device_id_type=MESH
        )
    pl.semaphore_wait(barrier, len(peers))


TO_RIGHT = (False, True, True, False, False, True)


class Pieces:
    def __init__(self, send, recv, keep, own, send_sem, recv_sem):
        self.send, self.recv, self.keep, self.own = send, recv, keep, own
        self.send_sem, self.recv_sem = send_sem, recv_sem
        self.chunks, self.rows, self.wide = own.shape

    def copy(self, kind, c):
        me, right, opposite, left = neighbours()
        return pltpu.make_async_remote_copy(
            src_ref=self.send.at[kind, c],
            dst_ref=self.recv.at[kind, c],
            send_sem=self.send_sem.at[kind, c],
            recv_sem=self.recv_sem.at[kind, c],
            device_id={"tensoror": right if TO_RIGHT[kind] else left},
            device_id_type=MESH,
        )

    def first(self, c, part):
        me, right, opposite, left = neighbours()
        send, keep = self.send, self.keep
        half = self.rows // 2
        sums = part(2, opposite)
        send[0, c] = sums[:half].astype(jnp.bfloat16)
        send[1, c] = sums[half:].astype(jnp.bfloat16)
        self.copy(0, c).start()
        self.copy(1, c).start()
        sums = part(1, right)
        send[2, c] = sums[:half].astype(jnp.bfloat16)
        keep[1, c] = sums[half:]
        self.copy(2, c).start()
        sums = part(3, left)
        send[3, c] = sums[half:].astype(jnp.bfloat16)
        keep[0, c] = sums[:half]
        self.copy(3, c).start()
        self.own[c] = part(0, me)

    def pass_on(self, c):
        for side in (0, 1):
            self.copy(side, c).wait_recv()
            self.send[4 + side, c] = (
                self.keep[side, c] + self.recv[side, c].astype(jnp.float32)
            ).astype(jnp.bfloat16)
            self.copy(4 + side, c).start()

    def last(self, c):
        for kind in (2, 3, 4, 5):
            self.copy(kind, c).wait_recv()
        half = self.rows // 2
        own, recv = self.own, self.recv
        return [
            own[c, side * half : (side + 1) * half]
            + recv[2 + side, c].astype(jnp.float32)
            + recv[4 + side, c].astype(jnp.float32)
            for side in (0, 1)
        ]

    def finish(self):
        def wait(c):
            for kind in range(6):
                self.copy(kind, c).wait_send()

        each(0, self.chunks, wait)


def each(start, stop, body):
    lax.fori_loop(start, stop, lambda c, _: (body(c), 0)[1], 0)


def piece_scratch(chunks, rows, wide):
    return [
        pltpu.VMEM((6, chunks, rows // 2, wide), jnp.bfloat16),
        pltpu.VMEM((6, chunks, rows // 2, wide), jnp.bfloat16),
        pltpu.VMEM((2, chunks, rows // 2, wide), jnp.float32),
        pltpu.VMEM((chunks, rows, wide), jnp.float32),
        pltpu.SemaphoreType.DMA((6, chunks)),
        pltpu.SemaphoreType.DMA((6, chunks)),
    ]


def project_kernel(act_ref, w_ref, out_ref, weights, weight_sem, *scratch):
    me, right, opposite, left = neighbours()
    pieces = Pieces(*scratch)
    chunks, rows, wide = pieces.own.shape

    def load(k, dest, c):
        column = pl.multiple_of(dest * (chunks * wide) + c * wide, 128)
        return pltpu.make_async_copy(
            w_ref.at[:, pl.ds(column, wide)], weights.at[k, c], weight_sem.at[k, c]
        )

    for c in range(chunks):
        for k, dest in ((2, opposite), (1, right), (3, left), (0, me)):
            load(k, dest, c).start()
    greet([{"tensoror": peer} for peer in (left, right)])

    def first(c):
        def part(k, dest):
            load(k, dest, c).wait()
            return jnp.dot(act_ref[...], weights[k, c], preferred_element_type=jnp.float32)

        pieces.first(c, part)

    def last(c):
        column = pl.ds(pl.multiple_of(c * wide, 128), wide)
        for side, sums in enumerate(pieces.last(c)):
            half = rows // 2
            out_ref[side * half : (side + 1) * half, column] = sums.astype(jnp.bfloat16)

    each(0, chunks, first)
    each(0, chunks, pieces.pass_on)
    each(0, chunks, last)
    pieces.finish()


def project(activated, weight):
    rows, depth = activated.shape
    width = weight.shape[1] // lax.axis_size("tensoror")
    wide = 256
    chunks = width // wide
    return pl.pallas_call(
        project_kernel,
        in_specs=[
            pl.BlockSpec(memory_space=pltpu.VMEM),
            pl.BlockSpec(memory_space=pl.ANY),
        ],
        out_specs=pl.BlockSpec(memory_space=pltpu.VMEM),
        out_shape=jax.ShapeDtypeStruct((rows, width), jnp.bfloat16),
        scratch_shapes=[
            pltpu.VMEM((4, chunks, depth, wide), jnp.bfloat16),
            pltpu.SemaphoreType.DMA((4, chunks)),
        ]
        + piece_scratch(chunks, rows, wide),
        compiler_params=pltpu.CompilerParams(
            collective_id=1, has_side_effects=True, vmem_limit_bytes=VMEM
        ),
    )(activated, weight)


OWN, NEXT, PREV, ACROSS, PARTNER = (0, 0, 0), (1, 0, 0), (3, 0, 0), (0, 1, 0), (0, 0, 1)
FAR = (2, 0, 0)
KINDS = {
    "next": (OWN, PREV, None),
    "prev": (OWN, NEXT, None),
    "across": (OWN, ACROSS, None),
    "partner": (OWN, PARTNER, None),
    "far0": (NEXT, PREV, 0),
    "far1": (PREV, NEXT, 1),
    "next_across": (ACROSS, PREV, None),
    "prev_across": (ACROSS, NEXT, None),
    "far_across0": (FAR, ACROSS, 0),
    "far_across1": (FAR, ACROSS, 1),
}
GOT = {
    "next": NEXT,
    "prev": PREV,
    "across": ACROSS,
    "partner": PARTNER,
    "far0": FAR,
    "far1": FAR,
    "next_across": (1, 1, 0),
    "prev_across": (3, 1, 0),
    "far_across0": (2, 1, 0),
    "far_across1": (2, 1, 0),
}
for name in list(GOT):
    if name != "partner":
        KINDS["twin_" + name] = (GOT[name], PARTNER, KINDS[name][2])
        GOT["twin_" + name] = GOT[name][:2] + (1,)
ORDER = {name: k for k, name in enumerate(KINDS)}


def seq_at(offset):
    place = lax.axis_index("seq")
    y = lax.rem(lax.div(place, 4) + offset[0], 4)
    z = lax.rem(lax.div(place, 2) + offset[1], 2)
    core = lax.rem(place + offset[2], 2)
    return y * 4 + z * 2 + core


class Gather:
    def __init__(self, own_ref, blocks, send_sem, recv_sem):
        self.refs = own_ref, blocks, send_sem, recv_sem

    def copy(self, name, arrival):
        own_ref, blocks, send_sem, recv_sem = self.refs
        block, target, half = KINDS[name]
        rows = blocks.shape[1]
        cut = pl.ds(0, rows) if half is None else pl.ds(half * (rows // 2), rows // 2)
        where = blocks.at[seq_at(GOT[name] if arrival else block), cut]
        source = own_ref if block == OWN and not arrival and own_ref is not None else where
        k = ORDER[name]
        return pltpu.make_async_remote_copy(
            src_ref=source,
            dst_ref=where,
            send_sem=send_sem.at[k],
            recv_sem=recv_sem.at[k],
            device_id={"seq": seq_at(target)},
            device_id_type=MESH,
        )

    def start(self, *names):
        for name in names:
            self.copy(name, False).start()

    def arrived(self, *names):
        for name in names:
            self.copy(name, True).wait_recv()

    def finish(self):
        for name in KINDS:
            self.copy(name, False).wait_send()


def seq_peers():
    return [{"seq": seq_at(offset)} for offset in (NEXT, PREV, ACROSS, PARTNER)]


GATHER_SEMAPHORES = [
    pltpu.SemaphoreType.DMA((len(KINDS),)),
    pltpu.SemaphoreType.DMA((len(KINDS),)),
]


def mix_kernel(
    start_ref,
    count_ref,
    visual_ref,
    text_ref,
    gain_ref,
    out_ref,
    square_ref,
    blocks,
    text,
    text_send,
    text_recv,
    own_sem,
    send_sem,
    recv_sem,
):
    me, right, opposite, left = neighbours()
    group = lax.axis_index("group")
    place = lax.axis_index("seq")
    local = text_ref.shape[0]
    sequences, rows, width = text.shape
    part = blocks.shape[1] // sequences
    gather = Gather(visual_ref, blocks, send_sem, recv_sem)

    def columns(peer):
        return text_ref.at[:, :, pl.ds(pl.multiple_of(peer * width, 128), width)]

    own_text = pltpu.make_async_copy(columns(me), text.at[pl.ds(me * local, local)], own_sem)
    own_text.start()
    greet([{"tensoror": peer} for peer in (right, opposite, left)] + seq_peers())
    gather.start("next", "prev", "across", "partner")
    exchanges = []
    for k, peer in ((2, opposite), (1, right), (3, left)):
        exchanges.append(
            pltpu.make_async_remote_copy(
                src_ref=columns(peer),
                dst_ref=text.at[pl.ds(me * local, local)],
                send_sem=text_send.at[k],
                recv_sem=text_recv.at[k],
                device_id={"tensoror": peer},
                device_id_type=MESH,
            )
        )
    for exchange in exchanges:
        exchange.start()
    blocks[place] = visual_ref[...]
    gather.arrived("next")
    gather.start("far0", "twin_next")
    gather.arrived("prev")
    gather.start("far1", "twin_prev")
    gather.arrived("across")
    gather.start("next_across", "prev_across", "twin_across")
    gather.arrived("far0")
    gather.start("far_across0", "twin_far0")
    gather.arrived("far1")
    gather.start("far_across1", "twin_far1")
    gather.arrived("next_across")
    gather.start("twin_next_across")
    gather.arrived("prev_across")
    gather.start("twin_prev_across")
    gather.arrived("far_across0")
    gather.start("twin_far_across0")
    gather.arrived("far_across1")
    gather.start("twin_far_across1")
    gather.arrived("partner", *[name for name in KINDS if name.startswith("twin_")])
    own_text.wait()
    for exchange in exchanges:
        exchange.wait()
    diagonal = lax.broadcasted_iota(jnp.int32, (rows, rows), 0) == lax.broadcasted_iota(
        jnp.int32, (rows, rows), 1
    )

    def one(i):
        start = start_ref[group * sequences + i]
        slots = TILE * count_ref[group * sequences + i]
        visual = blocks[:, pl.ds(pl.multiple_of(i * part, part), part), :].reshape(-1, width)
        total = visual.shape[0]
        shift = place * rows - start
        slot = shift + lax.broadcasted_iota(jnp.int32, (rows, total), 0)
        column = lax.broadcasted_iota(jnp.int32, (rows, total), 1)
        pick = jnp.where((slot == column) & (column < slots), 1.0, 0.0).astype(jnp.bfloat16)
        placed = jnp.dot(pick, visual, preferred_element_type=jnp.float32)
        own = shift + lax.broadcasted_iota(jnp.int32, (rows, width), 0)
        inside = (own >= 0) & (own < slots)
        mixed = jnp.where(inside, placed, text[i].astype(jnp.float32))
        squares = jnp.sum(mixed * mixed, axis=1, keepdims=True)
        square_ref[pl.ds(i, 1), :] = jnp.sum(
            jnp.where(diagonal, squares, 0.0), axis=0, keepdims=True
        )
        out_ref[pl.ds(pl.multiple_of(i * rows, rows), rows), :] = (mixed * gain_ref[...]).astype(
            jnp.bfloat16
        )

    each(0, sequences, one)
    gather.finish()


def mix(starts, counts, visual, text, gain):
    devices = lax.axis_size("seq")
    count = lax.axis_size("tensoror")
    local, rows, full = text.shape
    width = full // count
    sequences = local * count
    smem = pl.BlockSpec(memory_space=pltpu.SMEM)
    vmem = pl.BlockSpec(memory_space=pltpu.VMEM)
    return pl.pallas_call(
        mix_kernel,
        in_specs=[smem, smem, vmem, pl.BlockSpec(memory_space=pl.ANY), vmem],
        out_specs=[vmem, vmem],
        out_shape=[
            jax.ShapeDtypeStruct((sequences * rows, width), jnp.bfloat16),
            jax.ShapeDtypeStruct((sequences, rows), jnp.float32),
        ],
        scratch_shapes=[
            pltpu.VMEM((devices,) + visual.shape, jnp.bfloat16),
            pltpu.VMEM((sequences, rows, width), jnp.bfloat16),
            pltpu.SemaphoreType.DMA((4,)),
            pltpu.SemaphoreType.DMA((4,)),
            pltpu.SemaphoreType.DMA,
        ]
        + GATHER_SEMAPHORES,
        compiler_params=pltpu.CompilerParams(
            collective_id=0, has_side_effects=True, vmem_limit_bytes=VMEM
        ),
    )(starts, counts, visual, text, gain)


def attend_kernel(
    x_ref,
    square_ref,
    wkv_ref,
    wq_ref,
    out_ref,
    kv_weights,
    q_weights,
    squares,
    total_squares,
    scale,
    blocks,
    queries,
    totals,
    kv_weight_sem,
    q_weight_sem,
    square_send,
    square_recv,
    gather_send,
    gather_recv,
    *scratch,
    width,
):
    me, right, opposite, left = neighbours()
    place = lax.axis_index("seq")
    chip = lax.div(place, 2)
    kv_pieces, q_pieces = Pieces(*scratch[:6]), Pieces(*scratch[6:])
    rows = HEAD_SIZE
    local = kv_pieces.rows // rows
    factor = math.log2(math.e) / math.sqrt(HEAD_SIZE)
    gather = Gather(None, blocks, gather_send, gather_recv)

    def weight_copy(source, c, wide, weights, sem):
        column = pl.ds(pl.multiple_of(c * wide, 128), wide)
        return pltpu.make_async_copy(source.at[:, column], weights.at[c], sem.at[c])

    def kv_copy(c):
        return weight_copy(wkv_ref, c, kv_pieces.wide, kv_weights, kv_weight_sem)

    def q_copy(c):
        return weight_copy(wq_ref, c, q_pieces.wide, q_weights, q_weight_sem)

    for c in range(kv_pieces.chunks):
        kv_copy(c).start()
    for c in range(q_pieces.chunks):
        q_copy(c).start()
    greet([{"tensoror": peer} for peer in (right, opposite, left)] + seq_peers())

    def square_copy(k, peer):
        return pltpu.make_async_remote_copy(
            src_ref=square_ref,
            dst_ref=squares.at[k],
            send_sem=square_send.at[k],
            recv_sem=square_recv.at[k],
            device_id={"tensoror": peer},
            device_id_type=MESH,
        )

    peers = ((1, right), (2, opposite), (3, left))
    for k, peer in peers:
        square_copy(k, peer).start()

    def part_of(weights, c):
        def part(k, dest):
            span = pl.ds(pl.multiple_of(dest * local * rows, rows), local * rows)
            return jnp.dot(x_ref[span, :], weights[c], preferred_element_type=jnp.float32)

        return part

    def first_kv(c):
        kv_copy(c).wait()
        kv_pieces.first(c, part_of(kv_weights, c))

    def first_q(c):
        q_copy(c).wait()
        q_pieces.first(c, part_of(q_weights, c))

    each(0, kv_pieces.chunks, first_kv)
    for k, peer in peers:
        square_copy(k, peer).wait()
    total_squares[...] = square_ref[...] + squares[1] + squares[2] + squares[3]
    diagonal = lax.broadcasted_iota(jnp.int32, (rows, rows), 0) == lax.broadcasted_iota(
        jnp.int32, (rows, rows), 1
    )
    for b in range(local):
        row = jnp.broadcast_to(total_squares[pl.ds(me * local + b, 1), :], (rows, rows))
        column = jnp.sum(jnp.where(diagonal, row, 0.0), axis=1, keepdims=True)
        scale[b * rows : (b + 1) * rows, :] = lax.rsqrt(column / width + epsilon)
    each(0, kv_pieces.chunks, kv_pieces.pass_on)
    each(0, 2, first_q)

    def last_kv(c):
        column = pl.ds(pl.multiple_of(c * kv_pieces.wide, 128), kv_pieces.wide)
        for b, sums in enumerate(kv_pieces.last(c)):
            span = slice(b * rows, (b + 1) * rows)
            blocks[place, span, column] = (sums * scale[span, :]).astype(jnp.bfloat16)

    each(0, kv_pieces.chunks, last_kv)
    gather.start("next", "prev", "across", "partner")

    def second_q(c):
        first_q(c)
        q_pieces.pass_on(c - 2)

    each(2, q_pieces.chunks, second_q)
    gather.arrived("next")
    gather.start("far0", "twin_next")
    gather.arrived("prev")
    gather.start("far1", "twin_prev")
    gather.arrived("across")
    gather.start("next_across", "prev_across", "twin_across")
    gather.arrived("far0")
    gather.start("far_across0", "twin_far0")
    gather.arrived("far1")
    gather.start("far_across1", "twin_far1")
    q_pieces.pass_on(2)
    gather.arrived("next_across")
    gather.start("twin_next_across")
    gather.arrived("prev_across")
    gather.start("twin_prev_across")
    gather.arrived("far_across0")
    gather.start("twin_far_across0")
    gather.arrived("far_across1")
    gather.start("twin_far_across1")
    q_pieces.pass_on(3)
    gather.arrived("partner", *[name for name in KINDS if name.startswith("twin_")])

    def absorb(b, h, other, state, masked):
        top, low = state
        span = slice(b * rows, (b + 1) * rows)
        pair = pl.ds(2 * other, 2)
        key_column = pl.multiple_of(h * HEAD_SIZE, 128)
        value_column = pl.multiple_of((h + KEY_VALUE_HEADS) * HEAD_SIZE, 128)
        keys = blocks[pair, span, pl.ds(key_column, HEAD_SIZE)]
        values = blocks[pair, span, pl.ds(value_column, HEAD_SIZE)]
        scores = lax.dot_general(
            keys.reshape(2 * rows, HEAD_SIZE),
            queries[b],
            (((1,), (1,)), ((), ())),
            preferred_element_type=jnp.float32,
        )
        if masked:
            key = lax.broadcasted_iota(jnp.int32, scores.shape, 0)
            query = (
                lax.rem(lax.broadcasted_iota(jnp.int32, scores.shape, 1), rows)
                + lax.rem(place, 2) * rows
            )
            scores = jnp.where(key <= query, scores, masked_score)
        best = jnp.max(scores, axis=0, keepdims=True)
        new = best if masked else jnp.maximum(top, best)
        expo = jnp.exp2((scores - new) * factor)
        summed = jnp.sum(expo, axis=0, keepdims=True)
        added = lax.dot_general(
            values.reshape(2 * rows, HEAD_SIZE),
            expo.astype(jnp.bfloat16),
            (((0,), (0,)), ((), ())),
            preferred_element_type=jnp.float32,
        )
        if masked:
            totals[b] = added
            return new, summed
        keep = jnp.exp2((top - new) * factor)
        totals[b] = totals[b] * keep + added
        return new, low * keep + summed

    def one_group(h):
        for b, sums in enumerate(q_pieces.last(h)):
            scaled = (sums * scale[b * rows : (b + 1) * rows, :]).astype(jnp.bfloat16)
            for j in range(GROUP_HEADS):
                queries[b, j * rows : (j + 1) * rows, :] = scaled[
                    :, j * HEAD_SIZE : (j + 1) * HEAD_SIZE
                ]
        states = tuple(absorb(b, h, chip, (None, None), True) for b in range(local))
        states = lax.fori_loop(
            0,
            chip,
            lambda other, now: tuple(absorb(b, h, other, now[b], False) for b in range(local)),
            states,
        )
        for b in range(local):
            result = totals[b] / states[b][1]
            for j in range(GROUP_HEADS):
                column = pl.multiple_of((h * GROUP_HEADS + j) * HEAD_SIZE, 128)
                out_ref[b * rows : (b + 1) * rows, pl.ds(column, HEAD_SIZE)] = jnp.transpose(
                    result[:, j * rows : (j + 1) * rows]
                ).astype(jnp.bfloat16)

    each(0, KEY_VALUE_HEADS, one_group)
    gather.finish()
    kv_pieces.finish()
    q_pieces.finish()


def attend(mixed, squares, kv_weight, q_weight, full_width):
    count = lax.axis_size("tensoror")
    devices = lax.axis_size("seq")
    total, width = mixed.shape
    rows = total // count
    kv_cols = kv_weight.shape[1]
    q_cols = q_weight.shape[1]
    kv_wide, q_wide = 512, GROUP_HEADS * HEAD_SIZE
    kv_chunks, q_chunks = kv_cols // kv_wide, q_cols // q_wide
    local = rows // HEAD_SIZE
    vmem = pl.BlockSpec(memory_space=pltpu.VMEM)
    hbm = pl.BlockSpec(memory_space=pl.ANY)
    return pl.pallas_call(
        functools.partial(attend_kernel, width=full_width),
        in_specs=[vmem, vmem, hbm, hbm],
        out_specs=vmem,
        out_shape=jax.ShapeDtypeStruct((rows, q_cols), jnp.bfloat16),
        scratch_shapes=[
            pltpu.VMEM((kv_chunks, width, kv_wide), jnp.bfloat16),
            pltpu.VMEM((q_chunks, width, q_wide), jnp.bfloat16),
            pltpu.VMEM((count,) + squares.shape, jnp.float32),
            pltpu.VMEM(squares.shape, jnp.float32),
            pltpu.VMEM((rows, 1), jnp.float32),
            pltpu.VMEM((devices, rows, kv_cols), jnp.bfloat16),
            pltpu.VMEM((local, q_wide, HEAD_SIZE), jnp.bfloat16),
            pltpu.VMEM((local, HEAD_SIZE, q_wide), jnp.float32),
            pltpu.SemaphoreType.DMA((kv_chunks,)),
            pltpu.SemaphoreType.DMA((q_chunks,)),
            pltpu.SemaphoreType.DMA((count,)),
            pltpu.SemaphoreType.DMA((count,)),
        ]
        + GATHER_SEMAPHORES
        + piece_scratch(kv_chunks, rows, kv_wide)
        + piece_scratch(q_chunks, rows, q_wide),
        compiler_params=pltpu.CompilerParams(
            collective_id=2, has_side_effects=True, vmem_limit_bytes=VMEM
        ),
    )(mixed, squares, kv_weight, q_weight)


def shards(
    visual_hidden,
    projector_weight,
    text_embeddings,
    tile_counts,
    image_start,
    norm_gain,
    query_weight,
    keyvalue_weight,
):
    sequence_local, extent_rows, width = text_embeddings.shape
    sequences, slot_rows, depth = visual_hidden.shape
    activated = jax.nn.gelu(visual_hidden.astype(jnp.float32), approximate=False).astype(
        jnp.bfloat16
    )
    visual = project(activated.reshape(sequences * slot_rows, depth), projector_weight)
    gain = lax.dynamic_slice_in_dim(norm_gain, lax.axis_index("tensoror") * depth, depth)
    mixed, squares = mix(image_start, tile_counts, visual, text_embeddings, gain.reshape(1, depth))
    context = attend(mixed, squares, keyvalue_weight, query_weight, width)
    return context.reshape(sequence_local, extent_rows, -1)


def solution(mesh):
    in_specs = (
        P("group", "seq", "tensoror"),
        P("tensoror", None),
        P(("group", "tensoror"), "seq", None),
        P(),
        P(),
        P(),
        P("tensoror", None),
        P("tensoror", None),
    )
    out_specs = P(("group", "tensoror"), "seq", None)
    return jax.shard_map(shards, mesh=mesh, in_specs=in_specs, out_specs=out_specs, check_vma=False)
```

time: 209 us -> 175 us (0.84)
  Pallas kernels: 200 us -> 165 us
    pallas_call x2 -> x1, Pallas kernels: 122 us -> 86.8 us  [attend(): pl.pallas_call(functools.partial(attend_kernel, width=full_width), in_spe...]
where the time goes in v3:
time: 175 us; the launch traced here: 173 us
  Pallas kernels  165 us (94%)
  other arithmetic  4.55 us (3%)
  local copies, waits for them, and re-layouts  3.82 us (2%)
    pallas_call x1, Pallas kernels, attend(): pl.pallas_call(functools.partial(attend_kernel, width=full_width), in_spe...  86.8 us
    pallas_call x1, Pallas kernels, mix(): pl.pallas_call(mix_kernel, in_specs=[smem, smem, vmem, pl.BlockSpec(memor...  49.7 us
    pallas_call x1, Pallas kernels, project(): pl.pallas_call(project_kernel, in_specs=[pl.BlockSpec(memory_space=pltpu....  28.2 us
    convert_element_type x1, other arithmetic, shards(): jax.nn.gelu(visual_hidden.astype(jnp.float32), approximate=False)  4.55 us

profile of v3, /device:TPU:57, one launch (start us, length us, event | category | flops | bytes accessed | tf_op | source)
XLA Modules:
  0.0 173.1 jit_solution(13065117039042557771)
XLA Ops:
  0.0 0.8 dynamic_slice.3
  0.8 0.6 reshape.10.gain_ref
  1.4 4.5 %fusion.1 = bf16[8,32,1280]{2,1,0:T(8,128)(2,1)} fusion(bf16[8,32,1280]{2,1,0:T(8,128)(2,1)} %param.8), kind=kLoop, calls=%fused_computation.4 | loop fusion | flops 21626880 | bytes 1310720 | tf_op jit(solution)/shard_map/convert_element_type | solution.py:636
  5.9 28.2 %shard_map.82.visual_ref = bf16[256,1280]{1,0:T(8,128)(2,1)} custom-call(bf16[256,1280]{1,0:T(8,128)(2,1)} %bitcast.3, bf16[1280,5120]{1,0:T(8,128)(2,1)} %w_ref.1), custom_call_target="tpu_custom_call" | custom-call | tf_op jit(solution)/shard_map/pallas_call | solution.py:160
  34.2 49.7 %shard_map.83 = (bf16[1024,1280]{1,0:T(8,128)(2,1)}, f32[8,128]{1,0:T(8,128)}) custom-call(s32[16]{0:T(128)} %start_ref.1, s32[16]{0:T(128)} %count_ref.1, bf16[256,1280]{1,0:T(8,128)(2,1)} %shard_map.82.visual_ref, bf16[2,128,5120]{2,1,0:T(8,128)(2,1)} %text_ref.1, f32[1,1280]{1,0:T(1,128)} %reshape.10.gain_ref), custom_call_target="tpu_custom_call" | custom-call | tf_op jit(solution)/shard_map/pallas_call | solution.py:369
  83.8 86.8 %shard_map.84 = bf16[256,2560]{1,0:T(8,128)(2,1)} custom-call(bf16[1024,1280]{1,0:T(8,128)(2,1)} %get-tuple-element.7.x_ref, f32[8,128]{1,0:T(8,128)} %get-tuple-element.8.square_ref, bf16[1280,1024]{1,0:T(8,128)(2,1)} %wkv_ref.1, bf16[1280,2560]{1,0:T(8,128)(2,1)} %wq_ref.1), custom_call_target="tpu_custom_call" | custom-call | tf_op jit(solution)/shard_map/pallas_call | solution.py:596
  170.6 2.5 %copy.10 = bf16[2,128,2560]{2,1,0:T(8,128)(2,1)} copy(bf16[2,128,2560]{2,1,0:T(8,128)(2,1)} %bitcast.2) | data formatting | bytes 2621440

commit v4 on v3

--- a/solution.py
+++ b/solution.py
@@ -115,65 +115,6 @@
         pltpu.SemaphoreType.DMA((6, chunks)),
         pltpu.SemaphoreType.DMA((6, chunks)),
     ]
-
-
-def project_kernel(act_ref, w_ref, out_ref, weights, weight_sem, *scratch):
-    me, right, opposite, left = neighbours()
-    pieces = Pieces(*scratch)
-    chunks, rows, wide = pieces.own.shape
-
-    def load(k, dest, c):
-        column = pl.multiple_of(dest * (chunks * wide) + c * wide, 128)
-        return pltpu.make_async_copy(
-            w_ref.at[:, pl.ds(column, wide)], weights.at[k, c], weight_sem.at[k, c]
-        )
-
-    for c in range(chunks):
-        for k, dest in ((2, opposite), (1, right), (3, left), (0, me)):
-            load(k, dest, c).start()
-    greet([{"tensoror": peer} for peer in (left, right)])
-
-    def first(c):
-        def part(k, dest):
-            load(k, dest, c).wait()
-            return jnp.dot(act_ref[...], weights[k, c], preferred_element_type=jnp.float32)
-
-        pieces.first(c, part)
-
-    def last(c):
-        column = pl.ds(pl.multiple_of(c * wide, 128), wide)
-        for side, sums in enumerate(pieces.last(c)):
-            half = rows // 2
-            out_ref[side * half : (side + 1) * half, column] = sums.astype(jnp.bfloat16)
-
-    each(0, chunks, first)
-    each(0, chunks, pieces.pass_on)
-    each(0, chunks, last)
-    pieces.finish()
-
-
-def project(activated, weight):
-    rows, depth = activated.shape
-    width = weight.shape[1] // lax.axis_size("tensoror")
-    wide = 256
-    chunks = width // wide
-    return pl.pallas_call(
-        project_kernel,
-        in_specs=[
-            pl.BlockSpec(memory_space=pltpu.VMEM),
-            pl.BlockSpec(memory_space=pl.ANY),
-        ],
-        out_specs=pl.BlockSpec(memory_space=pltpu.VMEM),
-        out_shape=jax.ShapeDtypeStruct((rows, width), jnp.bfloat16),
-        scratch_shapes=[
-            pltpu.VMEM((4, chunks, depth, wide), jnp.bfloat16),
-            pltpu.SemaphoreType.DMA((4, chunks)),
-        ]
-        + piece_scratch(chunks, rows, wide),
-        compiler_params=pltpu.CompilerParams(
-            collective_id=1, has_side_effects=True, vmem_limit_bytes=VMEM
-        ),
-    )(activated, weight)
 
 
 OWN, NEXT, PREV, ACROSS, PARTNER = (0, 0, 0), (1, 0, 0), (3, 0, 0), (0, 1, 0), (0, 0, 1)
@@ -218,19 +159,21 @@
 
 
 class Gather:
-    def __init__(self, own_ref, blocks, send_sem, recv_sem):
-        self.refs = own_ref, blocks, send_sem, recv_sem
+    def __init__(self, blocks, send_sem, recv_sem, first=0, last=None):
+        self.refs = blocks, send_sem, recv_sem
+        self.first, self.size = first, (last or blocks.shape[2]) - first
 
     def copy(self, name, arrival):
-        own_ref, blocks, send_sem, recv_sem = self.refs
+        blocks, send_sem, recv_sem = self.refs
         block, target, half = KINDS[name]
         rows = blocks.shape[1]
         cut = pl.ds(0, rows) if half is None else pl.ds(half * (rows // 2), rows // 2)
-        where = blocks.at[seq_at(GOT[name] if arrival else block), cut]
-        source = own_ref if block == OWN and not arrival and own_ref is not None else where
+        where = blocks.at[
+            seq_at(GOT[name] if arrival else block), cut, pl.ds(self.first, self.size)
+        ]
         k = ORDER[name]
         return pltpu.make_async_remote_copy(
-            src_ref=source,
+            src_ref=where,
             dst_ref=where,
             send_sem=send_sem.at[k],
             recv_sem=recv_sem.at[k],
@@ -261,131 +204,227 @@
 ]
 
 
+SPLIT = 512
+
+
 def mix_kernel(
     start_ref,
     count_ref,
-    visual_ref,
+    hidden_ref,
+    w_ref,
     text_ref,
     gain_ref,
     out_ref,
     square_ref,
+    act,
+    weights,
     blocks,
     text,
+    weight_sem,
     text_send,
     text_recv,
     own_sem,
-    send_sem,
-    recv_sem,
+    first_send,
+    first_recv,
+    second_send,
+    second_recv,
+    *scratch,
 ):
     me, right, opposite, left = neighbours()
     group = lax.axis_index("group")
     place = lax.axis_index("seq")
+    pieces = Pieces(*scratch)
+    chunks, wide = pieces.chunks, pieces.wide
     local = text_ref.shape[0]
     sequences, rows, width = text.shape
-    part = blocks.shape[1] // sequences
-    gather = Gather(visual_ref, blocks, send_sem, recv_sem)
-
-    def columns(peer):
-        return text_ref.at[:, :, pl.ds(pl.multiple_of(peer * width, 128), width)]
-
-    own_text = pltpu.make_async_copy(columns(me), text.at[pl.ds(me * local, local)], own_sem)
+    part_rows = blocks.shape[1] // sequences
+    early = SPLIT // wide
+    spans = ((0, SPLIT), (SPLIT, width))
+    gathers = (
+        Gather(blocks, first_send, first_recv, *spans[0]),
+        Gather(blocks, second_send, second_recv, *spans[1]),
+    )
+
+    def load(k, dest, c):
+        column = pl.multiple_of(dest * width + c * wide, 128)
+        return pltpu.make_async_copy(
+            w_ref.at[:, pl.ds(column, wide)], weights.at[k, c], weight_sem.at[k, c]
+        )
+
+    for c in range(chunks):
+        for k, dest in ((2, opposite), (1, right), (3, left), (0, me)):
+            load(k, dest, c).start()
+    own_text = pltpu.make_async_copy(
+        text_ref.at[:, :, pl.ds(pl.multiple_of(me * width, 128), width)],
+        text.at[pl.ds(me * local, local)],
+        own_sem,
+    )
     own_text.start()
     greet([{"tensoror": peer} for peer in (right, opposite, left)] + seq_peers())
-    gather.start("next", "prev", "across", "partner")
-    exchanges = []
-    for k, peer in ((2, opposite), (1, right), (3, left)):
-        exchanges.append(
-            pltpu.make_async_remote_copy(
-                src_ref=columns(peer),
-                dst_ref=text.at[pl.ds(me * local, local)],
-                send_sem=text_send.at[k],
-                recv_sem=text_recv.at[k],
-                device_id={"tensoror": peer},
-                device_id_type=MESH,
-            )
-        )
-    for exchange in exchanges:
-        exchange.start()
-    blocks[place] = visual_ref[...]
-    gather.arrived("next")
-    gather.start("far0", "twin_next")
-    gather.arrived("prev")
-    gather.start("far1", "twin_prev")
-    gather.arrived("across")
-    gather.start("next_across", "prev_across", "twin_across")
-    gather.arrived("far0")
-    gather.start("far_across0", "twin_far0")
-    gather.arrived("far1")
-    gather.start("far_across1", "twin_far1")
-    gather.arrived("next_across")
-    gather.start("twin_next_across")
-    gather.arrived("prev_across")
-    gather.start("twin_prev_across")
-    gather.arrived("far_across0")
-    gather.start("twin_far_across0")
-    gather.arrived("far_across1")
-    gather.start("twin_far_across1")
-    gather.arrived("partner", *[name for name in KINDS if name.startswith("twin_")])
-    own_text.wait()
-    for exchange in exchanges:
-        exchange.wait()
+
+    def exchange(k, peer, b, p):
+        first, last = spans[p]
+        source = pl.ds(pl.multiple_of(peer * width + first, 128), last - first)
+        return pltpu.make_async_remote_copy(
+            src_ref=text_ref.at[b, :, source],
+            dst_ref=text.at[me * local + b, :, pl.ds(first, last - first)],
+            send_sem=text_send.at[k, b, p],
+            recv_sem=text_recv.at[k, b, p],
+            device_id={"tensoror": peer},
+            device_id_type=MESH,
+        )
+
+    peers = ((2, opposite), (1, right), (3, left))
+    for k, peer in peers:
+        exchange(k, peer, 0, 0).start()
+    hidden = hidden_ref[...].astype(jnp.float32)
+    act[...] = (0.5 * hidden * (1.0 + lax.erf(hidden * math.sqrt(0.5)))).astype(jnp.bfloat16)
+
+    def first(c):
+        def part(k, dest):
+            load(k, dest, c).wait()
+            return jnp.dot(act[...], weights[k, c], preferred_element_type=jnp.float32)
+
+        pieces.first(c, part)
+
+    def last(c):
+        column = pl.ds(pl.multiple_of(c * wide, 128), wide)
+        half = pieces.rows // 2
+        for side, sums in enumerate(pieces.last(c)):
+            blocks[place, side * half : (side + 1) * half, column] = sums.astype(jnp.bfloat16)
+
+    def forward_near(gather):
+        gather.arrived("next")
+        gather.start("far0", "twin_next")
+        gather.arrived("prev")
+        gather.start("far1", "twin_prev")
+        gather.arrived("across")
+        gather.start("next_across", "prev_across", "twin_across")
+
+    def forward_far(gather):
+        gather.arrived("far0")
+        gather.start("far_across0", "twin_far0")
+        gather.arrived("far1")
+        gather.start("far_across1", "twin_far1")
+
+    def forward_last(gather):
+        gather.arrived("next_across")
+        gather.start("twin_next_across")
+        gather.arrived("prev_across")
+        gather.start("twin_prev_across")
+        gather.arrived("far_across0")
+        gather.start("twin_far_across0")
+        gather.arrived("far_across1")
+        gather.start("twin_far_across1")
+
+    def all_here(gather):
+        gather.arrived("partner", *[name for name in KINDS if name.startswith("twin_")])
+
     diagonal = lax.broadcasted_iota(jnp.int32, (rows, rows), 0) == lax.broadcasted_iota(
         jnp.int32, (rows, rows), 1
     )
 
-    def one(i):
-        start = start_ref[group * sequences + i]
-        slots = TILE * count_ref[group * sequences + i]
-        visual = blocks[:, pl.ds(pl.multiple_of(i * part, part), part), :].reshape(-1, width)
-        total = visual.shape[0]
-        shift = place * rows - start
-        slot = shift + lax.broadcasted_iota(jnp.int32, (rows, total), 0)
-        column = lax.broadcasted_iota(jnp.int32, (rows, total), 1)
-        pick = jnp.where((slot == column) & (column < slots), 1.0, 0.0).astype(jnp.bfloat16)
-        placed = jnp.dot(pick, visual, preferred_element_type=jnp.float32)
-        own = shift + lax.broadcasted_iota(jnp.int32, (rows, width), 0)
-        inside = (own >= 0) & (own < slots)
-        mixed = jnp.where(inside, placed, text[i].astype(jnp.float32))
-        squares = jnp.sum(mixed * mixed, axis=1, keepdims=True)
-        square_ref[pl.ds(i, 1), :] = jnp.sum(
-            jnp.where(diagonal, squares, 0.0), axis=0, keepdims=True
-        )
-        out_ref[pl.ds(pl.multiple_of(i * rows, rows), rows), :] = (mixed * gain_ref[...]).astype(
-            jnp.bfloat16
-        )
-
-    each(0, sequences, one)
-    gather.finish()
-
-
-def mix(starts, counts, visual, text, gain):
+    def mix_columns(p):
+        low, high = spans[p]
+        gain = gain_ref[:, pl.ds(pl.multiple_of(me * width + low, 128), high - low)]
+
+        def one(i):
+            start = start_ref[group * sequences + i]
+            slots = TILE * count_ref[group * sequences + i]
+            visual = blocks[
+                :, pl.ds(pl.multiple_of(i * part_rows, part_rows), part_rows), low:high
+            ].reshape(-1, high - low)
+            total = visual.shape[0]
+            shift = place * rows - start
+            slot = shift + lax.broadcasted_iota(jnp.int32, (rows, total), 0)
+            column = lax.broadcasted_iota(jnp.int32, (rows, total), 1)
+            pick = jnp.where((slot == column) & (column < slots), 1.0, 0.0).astype(jnp.bfloat16)
+            placed = jnp.dot(pick, visual, preferred_element_type=jnp.float32)
+            own = shift + lax.broadcasted_iota(jnp.int32, placed.shape, 0)
+            inside = (own >= 0) & (own < slots)
+            mixed = jnp.where(inside, placed, text[i, :, low:high].astype(jnp.float32))
+            squares = jnp.sum(mixed * mixed, axis=1, keepdims=True)
+            line = jnp.sum(jnp.where(diagonal, squares, 0.0), axis=0, keepdims=True)
+            if p == 0:
+                square_ref[pl.ds(i, 1), :] = line
+            else:
+                square_ref[pl.ds(i, 1), :] += line
+            out_ref[pl.ds(pl.multiple_of(i * rows, rows), rows), low:high] = (
+                mixed * gain
+            ).astype(jnp.bfloat16)
+
+        each(0, sequences, one)
+
+    each(0, early, first)
+    each(0, early, pieces.pass_on)
+    each(early, chunks - 1, first)
+    each(0, early, last)
+    gathers[0].start("next", "prev", "across", "partner")
+    each(chunks - 1, chunks, first)
+    each(early, chunks, pieces.pass_on)
+    for b, p in ((1, 0), (0, 1), (1, 1)):
+        for k, peer in peers:
+            exchange(k, peer, b, p).start()
+    forward_near(gathers[0])
+    each(early, chunks, last)
+    gathers[1].start("next", "prev", "across", "partner")
+    forward_far(gathers[0])
+    forward_last(gathers[0])
+    all_here(gathers[0])
+    own_text.wait()
+    for b in range(local):
+        for k, peer in peers:
+            exchange(k, peer, b, 0).wait()
+    mix_columns(0)
+    forward_near(gathers[1])
+    forward_far(gathers[1])
+    forward_last(gathers[1])
+    for b in range(local):
+        for k, peer in peers:
+            exchange(k, peer, b, 1).wait()
+    all_here(gathers[1])
+    mix_columns(1)
+    for gather in gathers:
+        gather.finish()
+    pieces.finish()
+
+
+def mix(starts, counts, hidden, weight, text, gain):
     devices = lax.axis_size("seq")
     count = lax.axis_size("tensoror")
     local, rows, full = text.shape
     width = full // count
     sequences = local * count
+    wide = 256
+    chunks = width // wide
     smem = pl.BlockSpec(memory_space=pltpu.SMEM)
     vmem = pl.BlockSpec(memory_space=pltpu.VMEM)
+    hbm = pl.BlockSpec(memory_space=pl.ANY)
     return pl.pallas_call(
         mix_kernel,
-        in_specs=[smem, smem, vmem, pl.BlockSpec(memory_space=pl.ANY), vmem],
+        in_specs=[smem, smem, vmem, hbm, hbm, vmem],
         out_specs=[vmem, vmem],
         out_shape=[
             jax.ShapeDtypeStruct((sequences * rows, width), jnp.bfloat16),
             jax.ShapeDtypeStruct((sequences, rows), jnp.float32),
         ],
         scratch_shapes=[
-            pltpu.VMEM((devices,) + visual.shape, jnp.bfloat16),
+            pltpu.VMEM(hidden.shape, jnp.bfloat16),
+            pltpu.VMEM((count, chunks, width, wide), jnp.bfloat16),
+            pltpu.VMEM((devices, hidden.shape[0], width), jnp.bfloat16),
             pltpu.VMEM((sequences, rows, width), jnp.bfloat16),
-            pltpu.SemaphoreType.DMA((4,)),
-            pltpu.SemaphoreType.DMA((4,)),
+            pltpu.SemaphoreType.DMA((count, chunks)),
+            pltpu.SemaphoreType.DMA((count, local, 2)),
+            pltpu.SemaphoreType.DMA((count, local, 2)),
             pltpu.SemaphoreType.DMA,
         ]
-        + GATHER_SEMAPHORES,
+        + GATHER_SEMAPHORES
+        + GATHER_SEMAPHORES
+        + piece_scratch(chunks, hidden.shape[0], wide),
         compiler_params=pltpu.CompilerParams(
             collective_id=0, has_side_effects=True, vmem_limit_bytes=VMEM
         ),
-    )(starts, counts, visual, text, gain)
+    )(starts, counts, hidden, weight, text, gain)
 
 
 def attend_kernel(
@@ -418,7 +457,7 @@
     rows = HEAD_SIZE
     local = kv_pieces.rows // rows
     factor = math.log2(math.e) / math.sqrt(HEAD_SIZE)
-    gather = Gather(None, blocks, gather_send, gather_recv)
+    gather = Gather(blocks, gather_send, gather_recv)
 
     def weight_copy(source, c, wide, weights, sem):
         column = pl.ds(pl.multiple_of(c * wide, 128), wide)
@@ -633,12 +672,14 @@
 ):
     sequence_local, extent_rows, width = text_embeddings.shape
     sequences, slot_rows, depth = visual_hidden.shape
-    activated = jax.nn.gelu(visual_hidden.astype(jnp.float32), approximate=False).astype(
-        jnp.bfloat16
+    mixed, squares = mix(
+        image_start,
+        tile_counts,
+        visual_hidden.reshape(sequences * slot_rows, depth),
+        projector_weight,
+        text_embeddings,
+        norm_gain.reshape(1, width),
     )
-    visual = project(activated.reshape(sequences * slot_rows, depth), projector_weight)
-    gain = lax.dynamic_slice_in_dim(norm_gain, lax.axis_index("tensoror") * depth, depth)
-    mixed, squares = mix(image_start, tile_counts, visual, text_embeddings, gain.reshape(1, depth))
     context = attend(mixed, squares, keyvalue_weight, query_weight, width)
     return context.reshape(sequence_local, extent_rows, -1)
 

time: 175 us -> 169 us (0.966)
  other arithmetic: 4.55 us -> 0 us
    convert_element_type x1 -> x0, other arithmetic: 4.55 us -> none  [shards(): jax.nn.gelu(visual_hidden.astype(jnp.float32), approximate=False)]
    pallas_call x1, Pallas kernels: 86.8 us -> 90 us  [attend(): pl.pallas_call(functools.partial(attend_kernel, width=full_width), in_spe...]
    pallas_call x2 -> x1, Pallas kernels: 77.9 us -> 75.9 us  [mix(): pl.pallas_call(mix_kernel, in_specs=[smem, smem, vmem, hbm, hbm, vmem], o...]
where the time goes in v4:
time: 169 us; the launch traced here: 168 us
  Pallas kernels  166 us (98%)
  local copies, waits for them, and re-layouts  2.46 us (1%)
    pallas_call x1, Pallas kernels, attend(): pl.pallas_call(functools.partial(attend_kernel, width=full_width), in_spe...  90 us
    pallas_call x1, Pallas kernels, mix(): pl.pallas_call(mix_kernel, in_specs=[smem, smem, vmem, hbm, hbm, vmem], o...  75.9 us

profile of v4, /device:TPU:57, one launch (start us, length us, event | category | flops | bytes accessed | tf_op | source)
XLA Modules:
  0.0 168.4 jit_solution(3560263936074511340)
XLA Ops:
  0.0 75.9 %shard_map.82 = (bf16[1024,1280]{1,0:T(8,128)(2,1)}, f32[8,128]{1,0:T(8,128)}) custom-call(s32[16]{0:T(128)} %start_ref.1, s32[16]{0:T(128)} %count_ref.1, bf16[256,1280]{1,0:T(8,128)(2,1)} %bitcast.4, bf16[1280,5120]{1,0:T(8,128)(2,1)} %w_ref.1, bf16[2,128,5120]{2,1,0:T(8,128)(2,1)} %text_ref.1, f32[1,5120]{1,0:T(1,128)} %bitcast.5), custom_call_target="tpu_custom_call" | custom-call | tf_op jit(solution)/shard_map/pallas_call | solution.py:403
  75.9 90.0 %shard_map.83 = bf16[256,2560]{1,0:T(8,128)(2,1)} custom-call(bf16[1024,1280]{1,0:T(8,128)(2,1)} %get-tuple-element.7.x_ref, f32[8,128]{1,0:T(8,128)} %get-tuple-element.8.square_ref, bf16[1280,1024]{1,0:T(8,128)(2,1)} %wkv_ref.1, bf16[1280,2560]{1,0:T(8,128)(2,1)} %wq_ref.1), custom_call_target="tpu_custom_call" | custom-call | tf_op jit(solution)/shard_map/pallas_call | solution.py:635
  166.0 2.5 %copy.10 = bf16[2,128,2560]{2,1,0:T(8,128)(2,1)} copy(bf16[2,128,2560]{2,1,0:T(8,128)(2,1)} %bitcast.3) | data formatting | bytes 2621440

commit v5 on v4

--- a/solution.py
+++ b/solution.py
@@ -204,7 +204,7 @@
 ]
 
 
-SPLIT = 512
+PASSES = (0, 1, 3, 5)
 
 
 def mix_kernel(
@@ -224,10 +224,8 @@
     text_send,
     text_recv,
     own_sem,
-    first_send,
-    first_recv,
-    second_send,
-    second_recv,
+    gather_send,
+    gather_recv,
     *scratch,
 ):
     me, right, opposite, left = neighbours()
@@ -238,12 +236,11 @@
     local = text_ref.shape[0]
     sequences, rows, width = text.shape
     part_rows = blocks.shape[1] // sequences
-    early = SPLIT // wide
-    spans = ((0, SPLIT), (SPLIT, width))
-    gathers = (
-        Gather(blocks, first_send, first_recv, *spans[0]),
-        Gather(blocks, second_send, second_recv, *spans[1]),
-    )
+    spans = [(a * wide, b * wide) for a, b in zip(PASSES, PASSES[1:])]
+    gathers = [
+        Gather(blocks, gather_send.at[p], gather_recv.at[p], *span)
+        for p, span in enumerate(spans)
+    ]
 
     def load(k, dest, c):
         column = pl.multiple_of(dest * width + c * wide, 128)
@@ -355,35 +352,50 @@
 
         each(0, sequences, one)
 
-    each(0, early, first)
-    each(0, early, pieces.pass_on)
-    each(early, chunks - 1, first)
-    each(0, early, last)
-    gathers[0].start("next", "prev", "across", "partner")
-    each(chunks - 1, chunks, first)
-    each(early, chunks, pieces.pass_on)
-    for b, p in ((1, 0), (0, 1), (1, 1)):
+    def own_start(p):
+        each(PASSES[p], PASSES[p + 1], last)
+        gathers[p].start("next", "prev", "across", "partner")
+
+    def text_here(p):
+        for b in range(local):
+            for k, peer in peers:
+                exchange(k, peer, b, p).wait()
+
+    each(0, 1, first)
+    each(1, 2, first)
+    each(0, 1, pieces.pass_on)
+    each(2, 3, first)
+    each(1, 2, pieces.pass_on)
+    own_start(0)
+    each(3, 4, first)
+    each(2, 3, pieces.pass_on)
+    each(4, 5, first)
+    each(3, 4, pieces.pass_on)
+    forward_near(gathers[0])
+    own_start(1)
+    each(4, 5, pieces.pass_on)
+    for b, p in ((1, 0), (0, 1), (1, 1), (0, 2), (1, 2)):
         for k, peer in peers:
             exchange(k, peer, b, p).start()
-    forward_near(gathers[0])
-    each(early, chunks, last)
-    gathers[1].start("next", "prev", "across", "partner")
     forward_far(gathers[0])
     forward_last(gathers[0])
+    forward_near(gathers[1])
+    own_start(2)
+    own_text.wait()
     all_here(gathers[0])
-    own_text.wait()
-    for b in range(local):
-        for k, peer in peers:
-            exchange(k, peer, b, 0).wait()
+    forward_far(gathers[1])
+    text_here(0)
     mix_columns(0)
-    forward_near(gathers[1])
-    forward_far(gathers[1])
     forward_last(gathers[1])
-    for b in range(local):
-        for k, peer in peers:
-            exchange(k, peer, b, 1).wait()
+    forward_near(gathers[2])
     all_here(gathers[1])
+    forward_far(gathers[2])
+    text_here(1)
     mix_columns(1)
+    forward_last(gathers[2])
+    text_here(2)
+    all_here(gathers[2])
+    mix_columns(2)
     for gather in gathers:
         gather.finish()
     pieces.finish()
@@ -414,12 +426,12 @@
             pltpu.VMEM((devices, hidden.shape[0], width), jnp.bfloat16),
             pltpu.VMEM((sequences, rows, width), jnp.bfloat16),
             pltpu.SemaphoreType.DMA((count, chunks)),
-            pltpu.SemaphoreType.DMA((count, local, 2)),
-            pltpu.SemaphoreType.DMA((count, local, 2)),
+            pltpu.SemaphoreType.DMA((count, local, len(PASSES) - 1)),
+            pltpu.SemaphoreType.DMA((count, local, len(PASSES) - 1)),
             pltpu.SemaphoreType.DMA,
+            pltpu.SemaphoreType.DMA((len(PASSES) - 1, len(KINDS))),
+            pltpu.SemaphoreType.DMA((len(PASSES) - 1, len(KINDS))),
         ]
-        + GATHER_SEMAPHORES
-        + GATHER_SEMAPHORES
         + piece_scratch(chunks, hidden.shape[0], wide),
         compiler_params=pltpu.CompilerParams(
             collective_id=0, has_side_effects=True, vmem_limit_bytes=VMEM
@@ -551,7 +563,6 @@
     gather.start("twin_far_across0")
     gather.arrived("far_across1")
     gather.start("twin_far_across1")
-    q_pieces.pass_on(3)
     gather.arrived("partner", *[name for name in KINDS if name.startswith("twin_")])
 
     def absorb(b, h, other, state, masked):
@@ -614,7 +625,9 @@
                     result[:, j * rows : (j + 1) * rows]
                 ).astype(jnp.bfloat16)
 
-    each(0, KEY_VALUE_HEADS, one_group)
+    each(0, 1, one_group)
+    q_pieces.pass_on(3)
+    each(1, KEY_VALUE_HEADS, one_group)
     gather.finish()
     kv_pieces.finish()
     q_pieces.finish()

time: 169 us -> 163 us (0.964)
  Pallas kernels: 166 us -> 161 us
    pallas_call x1, Pallas kernels: 75.9 us -> 67.6 us  [mix(): pl.pallas_call(mix_kernel, in_specs=[smem, smem, vmem, hbm, hbm, vmem], o...]
    pallas_call x1, Pallas kernels: 90 us -> 93 us  [attend(): pl.pallas_call(functools.partial(attend_kernel, width=full_width), in_spe...]
where the time goes in v5:
time: 163 us
  Pallas kernels  161 us (99%)
  local copies, waits for them, and re-layouts  2.46 us (2%)
    pallas_call x1, Pallas kernels, attend(): pl.pallas_call(functools.partial(attend_kernel, width=full_width), in_spe...  93 us
    pallas_call x1, Pallas kernels, mix(): pl.pallas_call(mix_kernel, in_specs=[smem, smem, vmem, hbm, hbm, vmem], o...  67.6 us

profile of v5, /device:TPU:57, one launch (start us, length us, event | category | flops | bytes accessed | tf_op | source)
XLA Modules:
  0.0 163.1 jit_solution(6851096970048507687)
XLA Ops:
  0.0 67.6 %shard_map.82 = (bf16[1024,1280]{1,0:T(8,128)(2,1)}, f32[8,128]{1,0:T(8,128)}) custom-call(s32[16]{0:T(128)} %start_ref.1, s32[16]{0:T(128)} %count_ref.1, bf16[256,1280]{1,0:T(8,128)(2,1)} %bitcast.4, bf16[1280,5120]{1,0:T(8,128)(2,1)} %w_ref.1, bf16[2,128,5120]{2,1,0:T(8,128)(2,1)} %text_ref.1, f32[1,5120]{1,0:T(1,128)} %bitcast.5), custom_call_target="tpu_custom_call" | custom-call | tf_op jit(solution)/shard_map/pallas_call | solution.py:415
  67.6 93.0 %shard_map.83 = bf16[256,2560]{1,0:T(8,128)(2,1)} custom-call(bf16[1024,1280]{1,0:T(8,128)(2,1)} %get-tuple-element.7.x_ref, f32[8,128]{1,0:T(8,128)} %get-tuple-element.8.square_ref, bf16[1280,1024]{1,0:T(8,128)(2,1)} %wkv_ref.1, bf16[1280,2560]{1,0:T(8,128)(2,1)} %wq_ref.1), custom_call_target="tpu_custom_call" | custom-call | tf_op jit(solution)/shard_map/pallas_call | solution.py:648
  160.6 2.5 %copy.10 = bf16[2,128,2560]{2,1,0:T(8,128)(2,1)} copy(bf16[2,128,2560]{2,1,0:T(8,128)(2,1)} %bitcast.3) | data formatting | bytes 2621440

commit v6 on v5

--- a/solution.py
+++ b/solution.py
@@ -120,8 +120,10 @@
 OWN, NEXT, PREV, ACROSS, PARTNER = (0, 0, 0), (1, 0, 0), (3, 0, 0), (0, 1, 0), (0, 0, 1)
 FAR = (2, 0, 0)
 KINDS = {
-    "next": (OWN, PREV, None),
-    "prev": (OWN, NEXT, None),
+    "next0": (OWN, PREV, 0),
+    "next1": (OWN, PREV, 1),
+    "prev1": (OWN, NEXT, 1),
+    "prev0": (OWN, NEXT, 0),
     "across": (OWN, ACROSS, None),
     "partner": (OWN, PARTNER, None),
     "far0": (NEXT, PREV, 0),
@@ -132,8 +134,10 @@
     "far_across1": (FAR, ACROSS, 1),
 }
 GOT = {
-    "next": NEXT,
-    "prev": PREV,
+    "next0": NEXT,
+    "next1": NEXT,
+    "prev1": PREV,
+    "prev0": PREV,
     "across": ACROSS,
     "partner": PARTNER,
     "far0": FAR,
@@ -148,6 +152,9 @@
         KINDS["twin_" + name] = (GOT[name], PARTNER, KINDS[name][2])
         GOT["twin_" + name] = GOT[name][:2] + (1,)
 ORDER = {name: k for k, name in enumerate(KINDS)}
+NEAR_TWINS = [
+    "twin_" + name for name in ("next0", "next1", "prev1", "prev0", "across", "far0", "far1")
+]
 
 
 def seq_at(offset):
@@ -188,6 +195,43 @@
     def arrived(self, *names):
         for name in names:
             self.copy(name, True).wait_recv()
+
+    def start_own(self):
+        self.start("next0", "prev1", "across", "next1", "prev0", "partner")
+
+    def forward_near(self):
+        self.arrived("next0")
+        self.start("far0", "twin_next0")
+        self.arrived("prev1")
+        self.start("far1", "twin_prev1")
+        self.arrived("across")
+        self.start("next_across", "prev_across", "twin_across")
+        self.arrived("next1")
+        self.start("twin_next1")
+        self.arrived("prev0")
+        self.start("twin_prev0")
+
+    def forward_far(self):
+        self.arrived("far0")
+        self.start("far_across0", "twin_far0")
+        self.arrived("far1")
+        self.start("far_across1", "twin_far1")
+
+    def forward_last(self):
+        self.arrived("next_across")
+        self.start("twin_next_across")
+        self.arrived("prev_across")
+        self.start("twin_prev_across")
+        self.arrived("far_across0")
+        self.start("twin_far_across0")
+        self.arrived("far_across1")
+        self.start("twin_far_across1")
+
+    def near_here(self):
+        self.arrived("partner", *[name for name in KINDS if name in NEAR_TWINS])
+
+    def late_here(self):
+        self.arrived(*[name for name in KINDS if name[:5] == "twin_" and name not in NEAR_TWINS])
 
     def finish(self):
         for name in KINDS:
@@ -290,33 +334,6 @@
         for side, sums in enumerate(pieces.last(c)):
             blocks[place, side * half : (side + 1) * half, column] = sums.astype(jnp.bfloat16)
 
-    def forward_near(gather):
-        gather.arrived("next")
-        gather.start("far0", "twin_next")
-        gather.arrived("prev")
-        gather.start("far1", "twin_prev")
-        gather.arrived("across")
-        gather.start("next_across", "prev_across", "twin_across")
-
-    def forward_far(gather):
-        gather.arrived("far0")
-        gather.start("far_across0", "twin_far0")
-        gather.arrived("far1")
-        gather.start("far_across1", "twin_far1")
-
-    def forward_last(gather):
-        gather.arrived("next_across")
-        gather.start("twin_next_across")
-        gather.arrived("prev_across")
-        gather.start("twin_prev_across")
-        gather.arrived("far_across0")
-        gather.start("twin_far_across0")
-        gather.arrived("far_across1")
-        gather.start("twin_far_across1")
-
-    def all_here(gather):
-        gather.arrived("partner", *[name for name in KINDS if name.startswith("twin_")])
-
     diagonal = lax.broadcasted_iota(jnp.int32, (rows, rows), 0) == lax.broadcasted_iota(
         jnp.int32, (rows, rows), 1
     )
@@ -354,7 +371,7 @@
 
     def own_start(p):
         each(PASSES[p], PASSES[p + 1], last)
-        gathers[p].start("next", "prev", "across", "partner")
+        gathers[p].start_own()
 
     def text_here(p):
         for b in range(local):
@@ -371,30 +388,33 @@
     each(2, 3, pieces.pass_on)
     each(4, 5, first)
     each(3, 4, pieces.pass_on)
-    forward_near(gathers[0])
+    gathers[0].forward_near()
     own_start(1)
     each(4, 5, pieces.pass_on)
     for b, p in ((1, 0), (0, 1), (1, 1), (0, 2), (1, 2)):
         for k, peer in peers:
             exchange(k, peer, b, p).start()
-    forward_far(gathers[0])
-    forward_last(gathers[0])
-    forward_near(gathers[1])
+    gathers[0].forward_far()
+    gathers[0].forward_last()
+    gathers[1].forward_near()
     own_start(2)
     own_text.wait()
-    all_here(gathers[0])
-    forward_far(gathers[1])
+    gathers[0].near_here()
+    gathers[0].late_here()
+    gathers[1].forward_far()
     text_here(0)
     mix_columns(0)
-    forward_last(gathers[1])
-    forward_near(gathers[2])
-    all_here(gathers[1])
-    forward_far(gathers[2])
+    gathers[1].forward_last()
+    gathers[2].forward_near()
+    gathers[1].near_here()
+    gathers[1].late_here()
+    gathers[2].forward_far()
     text_here(1)
     mix_columns(1)
-    forward_last(gathers[2])
+    gathers[2].forward_last()
     text_here(2)
-    all_here(gathers[2])
+    gathers[2].near_here()
+    gathers[2].late_here()
     mix_columns(2)
     for gather in gathers:
         gather.finish()
@@ -453,6 +473,8 @@
     blocks,
     queries,
     totals,
+    top,
+    low,
     kv_weight_sem,
     q_weight_sem,
     square_send,
@@ -537,36 +559,14 @@
             blocks[place, span, column] = (sums * scale[span, :]).astype(jnp.bfloat16)
 
     each(0, kv_pieces.chunks, last_kv)
-    gather.start("next", "prev", "across", "partner")
+    gather.start_own()
 
     def second_q(c):
         first_q(c)
         q_pieces.pass_on(c - 2)
 
-    each(2, q_pieces.chunks, second_q)
-    gather.arrived("next")
-    gather.start("far0", "twin_next")
-    gather.arrived("prev")
-    gather.start("far1", "twin_prev")
-    gather.arrived("across")
-    gather.start("next_across", "prev_across", "twin_across")
-    gather.arrived("far0")
-    gather.start("far_across0", "twin_far0")
-    gather.arrived("far1")
-    gather.start("far_across1", "twin_far1")
-    q_pieces.pass_on(2)
-    gather.arrived("next_across")
-    gather.start("twin_next_across")
-    gather.arrived("prev_across")
-    gather.start("twin_prev_across")
-    gather.arrived("far_across0")
-    gather.start("twin_far_across0")
-    gather.arrived("far_across1")
-    gather.start("twin_far_across1")
-    gather.arrived("partner", *[name for name in KINDS if name.startswith("twin_")])
-
-    def absorb(b, h, other, state, masked):
-        top, low = state
+    def absorb(b, h, other, masked):
+        unit = b * KEY_VALUE_HEADS + h
         span = slice(b * rows, (b + 1) * rows)
         pair = pl.ds(2 * other, 2)
         key_column = pl.multiple_of(h * HEAD_SIZE, 128)
@@ -575,7 +575,7 @@
         values = blocks[pair, span, pl.ds(value_column, HEAD_SIZE)]
         scores = lax.dot_general(
             keys.reshape(2 * rows, HEAD_SIZE),
-            queries[b],
+            queries[unit],
             (((1,), (1,)), ((), ())),
             preferred_element_type=jnp.float32,
         )
@@ -587,7 +587,7 @@
             )
             scores = jnp.where(key <= query, scores, masked_score)
         best = jnp.max(scores, axis=0, keepdims=True)
-        new = best if masked else jnp.maximum(top, best)
+        new = best if masked else jnp.maximum(top[unit], best)
         expo = jnp.exp2((scores - new) * factor)
         summed = jnp.sum(expo, axis=0, keepdims=True)
         added = lax.dot_general(
@@ -597,37 +597,69 @@
             preferred_element_type=jnp.float32,
         )
         if masked:
-            totals[b] = added
-            return new, summed
-        keep = jnp.exp2((top - new) * factor)
-        totals[b] = totals[b] * keep + added
-        return new, low * keep + summed
-
-    def one_group(h):
+            totals[unit] = added
+            low[unit] = summed
+        else:
+            keep = jnp.exp2((top[unit] - new) * factor)
+            totals[unit] = totals[unit] * keep + added
+            low[unit] = low[unit] * keep + summed
+        top[unit] = new
+
+    def absorb_other(h, steps, across):
+        other = lax.div(seq_at((steps, across, 0)), 2)
+
+        @pl.when(other < chip)
+        def _():
+            for b in range(local):
+                absorb(b, h, other, False)
+
+    def group_near(h):
         for b, sums in enumerate(q_pieces.last(h)):
+            unit = b * KEY_VALUE_HEADS + h
             scaled = (sums * scale[b * rows : (b + 1) * rows, :]).astype(jnp.bfloat16)
             for j in range(GROUP_HEADS):
-                queries[b, j * rows : (j + 1) * rows, :] = scaled[
+                queries[unit, j * rows : (j + 1) * rows, :] = scaled[
                     :, j * HEAD_SIZE : (j + 1) * HEAD_SIZE
                 ]
-        states = tuple(absorb(b, h, chip, (None, None), True) for b in range(local))
-        states = lax.fori_loop(
-            0,
-            chip,
-            lambda other, now: tuple(absorb(b, h, other, now[b], False) for b in range(local)),
-            states,
-        )
         for b in range(local):
-            result = totals[b] / states[b][1]
+            absorb(b, h, chip, True)
+        each(0, 4, lambda steps: absorb_other(h, steps, jnp.where(steps == 0, 1, 0)))
+
+    def group_late(h):
+        each(1, 4, lambda steps: absorb_other(h, steps, 1))
+        for b in range(local):
+            unit = b * KEY_VALUE_HEADS + h
+            result = totals[unit] / low[unit]
             for j in range(GROUP_HEADS):
                 column = pl.multiple_of((h * GROUP_HEADS + j) * HEAD_SIZE, 128)
                 out_ref[b * rows : (b + 1) * rows, pl.ds(column, HEAD_SIZE)] = jnp.transpose(
                     result[:, j * rows : (j + 1) * rows]
                 ).astype(jnp.bfloat16)
 
-    each(0, 1, one_group)
+    each(2, q_pieces.chunks, second_q)
+    gather.forward_near()
+    gather.forward_far()
+    q_pieces.pass_on(2)
+    gather.near_here()
+    each(0, 1, group_near)
+    gather.arrived("next_across")
+    gather.start("twin_next_across")
+    gather.arrived("prev_across")
+    gather.start("twin_prev_across")
+    each(1, 2, group_near)
+    gather.arrived("far_across0")
+    gather.start("twin_far_across0")
+    gather.arrived("far_across1")
+    gather.start("twin_far_across1")
     q_pieces.pass_on(3)
-    each(1, KEY_VALUE_HEADS, one_group)
+    gather.late_here()
+    each(0, 2, group_late)
+
+    def whole(h):
+        group_near(h)
+        group_late(h)
+
+    each(2, KEY_VALUE_HEADS, whole)
     gather.finish()
     kv_pieces.finish()
     q_pieces.finish()
@@ -657,8 +689,10 @@
             pltpu.VMEM(squares.shape, jnp.float32),
             pltpu.VMEM((rows, 1), jnp.float32),
             pltpu.VMEM((devices, rows, kv_cols), jnp.bfloat16),
-            pltpu.VMEM((local, q_wide, HEAD_SIZE), jnp.bfloat16),
-            pltpu.VMEM((local, HEAD_SIZE, q_wide), jnp.float32),
+            pltpu.VMEM((local * KEY_VALUE_HEADS, q_wide, HEAD_SIZE), jnp.bfloat16),
+            pltpu.VMEM((local * KEY_VALUE_HEADS, HEAD_SIZE, q_wide), jnp.float32),
+            pltpu.VMEM((local * KEY_VALUE_HEADS, 1, q_wide), jnp.float32),
+            pltpu.VMEM((local * KEY_VALUE_HEADS, 1, q_wide), jnp.float32),
             pltpu.SemaphoreType.DMA((kv_chunks,)),
             pltpu.SemaphoreType.DMA((q_chunks,)),
             pltpu.SemaphoreType.DMA((count,)),

time: 163 us -> 161 us (0.988)
  Pallas kernels: 161 us -> 158 us
    pallas_call x1, Pallas kernels: 93 us -> 89.9 us  [attend(): pl.pallas_call(functools.partial(attend_kernel, width=full_width), in_spe...]
where the time goes in v6:
time: 161 us
  Pallas kernels  158 us (98%)
  local copies, waits for them, and re-layouts  2.46 us (2%)
    pallas_call x1, Pallas kernels, attend(): pl.pallas_call(functools.partial(attend_kernel, width=full_width), in_spe...  89.9 us
    pallas_call x1, Pallas kernels, mix(): pl.pallas_call(mix_kernel, in_specs=[smem, smem, vmem, hbm, hbm, vmem], o...  68.4 us

profile of v6, /device:TPU:57, one launch (start us, length us, event | category | flops | bytes accessed | tf_op | source)
XLA Modules:
  0.0 160.7 jit_solution(4808904842003015899)
XLA Ops:
  0.0 68.4 %shard_map.82 = (bf16[1024,1280]{1,0:T(8,128)(2,1)}, f32[8,128]{1,0:T(8,128)}) custom-call(s32[16]{0:T(128)} %start_ref.1, s32[16]{0:T(128)} %count_ref.1, bf16[256,1280]{1,0:T(8,128)(2,1)} %bitcast.4, bf16[1280,5120]{1,0:T(8,128)(2,1)} %w_ref.1, bf16[2,128,5120]{2,1,0:T(8,128)(2,1)} %text_ref.1, f32[1,5120]{1,0:T(1,128)} %bitcast.5), custom_call_target="tpu_custom_call" | custom-call | tf_op jit(solution)/shard_map/pallas_call | solution.py:435
  68.4 89.9 %shard_map.83 = bf16[256,2560]{1,0:T(8,128)(2,1)} custom-call(bf16[1024,1280]{1,0:T(8,128)(2,1)} %get-tuple-element.7.x_ref, f32[8,128]{1,0:T(8,128)} %get-tuple-element.8.square_ref, bf16[1280,1024]{1,0:T(8,128)(2,1)} %wkv_ref.1, bf16[1280,2560]{1,0:T(8,128)(2,1)} %wq_ref.1), custom_call_target="tpu_custom_call" | custom-call | tf_op jit(solution)/shard_map/pallas_call | solution.py:680
  158.3 2.5 %copy.10 = bf16[2,128,2560]{2,1,0:T(8,128)(2,1)} copy(bf16[2,128,2560]{2,1,0:T(8,128)(2,1)} %bitcast.3) | data formatting | bytes 2621440

commit v7 on v6

--- a/solution.py
+++ b/solution.py
@@ -217,11 +217,13 @@
         self.arrived("far1")
         self.start("far_across1", "twin_far1")
 
-    def forward_last(self):
+    def forward_beside(self):
         self.arrived("next_across")
         self.start("twin_next_across")
         self.arrived("prev_across")
         self.start("twin_prev_across")
+
+    def forward_last(self):
         self.arrived("far_across0")
         self.start("twin_far_across0")
         self.arrived("far_across1")
@@ -230,8 +232,11 @@
     def near_here(self):
         self.arrived("partner", *[name for name in KINDS if name in NEAR_TWINS])
 
-    def late_here(self):
-        self.arrived(*[name for name in KINDS if name[:5] == "twin_" and name not in NEAR_TWINS])
+    def beside_here(self):
+        self.arrived("twin_next_across", "twin_prev_across")
+
+    def last_here(self):
+        self.arrived("twin_far_across0", "twin_far_across1")
 
     def finish(self):
         for name in KINDS:
@@ -395,26 +400,32 @@
         for k, peer in peers:
             exchange(k, peer, b, p).start()
     gathers[0].forward_far()
+    gathers[0].forward_beside()
     gathers[0].forward_last()
     gathers[1].forward_near()
     own_start(2)
     own_text.wait()
     gathers[0].near_here()
-    gathers[0].late_here()
+    gathers[0].beside_here()
+    gathers[0].last_here()
     gathers[1].forward_far()
     text_here(0)
     mix_columns(0)
+    gathers[1].forward_beside()
     gathers[1].forward_last()
     gathers[2].forward_near()
     gathers[1].near_here()
-    gathers[1].late_here()
+    gathers[1].beside_here()
+    gathers[1].last_here()
     gathers[2].forward_far()
     text_here(1)
     mix_columns(1)
+    gathers[2].forward_beside()
     gathers[2].forward_last()
     text_here(2)
     gathers[2].near_here()
-    gathers[2].late_here()
+    gathers[2].beside_here()
+    gathers[2].last_here()
     mix_columns(2)
     for gather in gathers:
         gather.finish()
@@ -625,8 +636,11 @@
             absorb(b, h, chip, True)
         each(0, 4, lambda steps: absorb_other(h, steps, jnp.where(steps == 0, 1, 0)))
 
-    def group_late(h):
-        each(1, 4, lambda steps: absorb_other(h, steps, 1))
+    def group_beside(h):
+        each(0, 2, lambda side: absorb_other(h, 1 + 2 * side, 1))
+
+    def group_last(h):
+        absorb_other(h, 2, 1)
         for b in range(local):
             unit = b * KEY_VALUE_HEADS + h
             result = totals[unit] / low[unit]
@@ -642,24 +656,18 @@
     q_pieces.pass_on(2)
     gather.near_here()
     each(0, 1, group_near)
-    gather.arrived("next_across")
-    gather.start("twin_next_across")
-    gather.arrived("prev_across")
-    gather.start("twin_prev_across")
+    gather.forward_beside()
     each(1, 2, group_near)
-    gather.arrived("far_across0")
-    gather.start("twin_far_across0")
-    gather.arrived("far_across1")
-    gather.start("twin_far_across1")
     q_pieces.pass_on(3)
-    gather.late_here()
-    each(0, 2, group_late)
-
-    def whole(h):
-        group_near(h)
-        group_late(h)
-
-    each(2, KEY_VALUE_HEADS, whole)
+    gather.beside_here()
+    each(0, 2, group_beside)
+    each(2, 3, group_near)
+    gather.forward_last()
+    each(2, 3, group_beside)
+    each(3, 4, group_near)
+    each(3, 4, group_beside)
+    gather.last_here()
+    each(0, KEY_VALUE_HEADS, group_last)
     gather.finish()
     kv_pieces.finish()
     q_pieces.finish()

time: 161 us -> 160 us (level)
  no operation moved by 1% of the time
where the time goes in v7:
time: 160 us
  Pallas kernels  157 us (98%)
  local copies, waits for them, and re-layouts  2.46 us (2%)
    pallas_call x1, Pallas kernels, attend(): pl.pallas_call(functools.partial(attend_kernel, width=full_width), in_spe...  88.8 us
    pallas_call x1, Pallas kernels, mix(): pl.pallas_call(mix_kernel, in_specs=[smem, smem, vmem, hbm, hbm, vmem], o...  68.4 us

profile of v7, /device:TPU:57, one launch (start us, length us, event | category | flops | bytes accessed | tf_op | source)
XLA Modules:
  0.0 159.6 jit_solution(17513765390109616576)
XLA Ops:
  0.0 68.4 %shard_map.82 = (bf16[1024,1280]{1,0:T(8,128)(2,1)}, f32[8,128]{1,0:T(8,128)}) custom-call(s32[16]{0:T(128)} %start_ref.1, s32[16]{0:T(128)} %count_ref.1, bf16[256,1280]{1,0:T(8,128)(2,1)} %bitcast.4, bf16[1280,5120]{1,0:T(8,128)(2,1)} %w_ref.1, bf16[2,128,5120]{2,1,0:T(8,128)(2,1)} %text_ref.1, f32[1,5120]{1,0:T(1,128)} %bitcast.5), custom_call_target="tpu_custom_call" | custom-call | tf_op jit(solution)/shard_map/pallas_call | solution.py:446
  68.4 88.8 %shard_map.83 = bf16[256,2560]{1,0:T(8,128)(2,1)} custom-call(bf16[1024,1280]{1,0:T(8,128)(2,1)} %get-tuple-element.7.x_ref, f32[8,128]{1,0:T(8,128)} %get-tuple-element.8.square_ref, bf16[1280,1024]{1,0:T(8,128)(2,1)} %wkv_ref.1, bf16[1280,2560]{1,0:T(8,128)(2,1)} %wq_ref.1), custom_call_target="tpu_custom_call" | custom-call | tf_op jit(solution)/shard_map/pallas_call | solution.py:688
  157.2 2.5 %copy.10 = bf16[2,128,2560]{2,1,0:T(8,128)(2,1)} copy(bf16[2,128,2560]{2,1,0:T(8,128)(2,1)} %bitcast.3) | data formatting | bytes 2621440

commit v8 on v7

--- a/solution.py
+++ b/solution.py
@@ -650,9 +650,11 @@
                     result[:, j * rows : (j + 1) * rows]
                 ).astype(jnp.bfloat16)
 
-    each(2, q_pieces.chunks, second_q)
+    each(0, 2, q_pieces.pass_on)
     gather.forward_near()
+    each(2, 3, first_q)
     gather.forward_far()
+    each(3, 4, first_q)
     q_pieces.pass_on(2)
     gather.near_here()
     each(0, 1, group_near)

time: 160 us -> 155 us (0.969)
  Pallas kernels: 157 us -> 152 us
    pallas_call x1, Pallas kernels: 88.8 us -> 83.9 us  [attend(): pl.pallas_call(functools.partial(attend_kernel, width=full_width), in_spe...]
where the time goes in v8:
time: 155 us
  Pallas kernels  152 us (98%)
  local copies, waits for them, and re-layouts  2.46 us (2%)
    pallas_call x1, Pallas kernels, attend(): pl.pallas_call(functools.partial(attend_kernel, width=full_width), in_spe...  83.9 us
    pallas_call x1, Pallas kernels, mix(): pl.pallas_call(mix_kernel, in_specs=[smem, smem, vmem, hbm, hbm, vmem], o...  68.4 us

profile of v8, /device:TPU:57, one launch (start us, length us, event | category | flops | bytes accessed | tf_op | source)
XLA Modules:
  0.0 154.8 jit_solution(16974404412620904056)
XLA Ops:
  0.0 68.4 %shard_map.82 = (bf16[1024,1280]{1,0:T(8,128)(2,1)}, f32[8,128]{1,0:T(8,128)}) custom-call(s32[16]{0:T(128)} %start_ref.1, s32[16]{0:T(128)} %count_ref.1, bf16[256,1280]{1,0:T(8,128)(2,1)} %bitcast.4, bf16[1280,5120]{1,0:T(8,128)(2,1)} %w_ref.1, bf16[2,128,5120]{2,1,0:T(8,128)(2,1)} %text_ref.1, f32[1,5120]{1,0:T(1,128)} %bitcast.5), custom_call_target="tpu_custom_call" | custom-call | tf_op jit(solution)/shard_map/pallas_call | solution.py:446
  68.4 83.9 %shard_map.83 = bf16[256,2560]{1,0:T(8,128)(2,1)} custom-call(bf16[1024,1280]{1,0:T(8,128)(2,1)} %get-tuple-element.7.x_ref, f32[8,128]{1,0:T(8,128)} %get-tuple-element.8.square_ref, bf16[1280,1024]{1,0:T(8,128)(2,1)} %wkv_ref.1, bf16[1280,2560]{1,0:T(8,128)(2,1)} %wq_ref.1), custom_call_target="tpu_custom_call" | custom-call | tf_op jit(solution)/shard_map/pallas_call | solution.py:690
  152.3 2.5 %copy.10 = bf16[2,128,2560]{2,1,0:T(8,128)(2,1)} copy(bf16[2,128,2560]{2,1,0:T(8,128)(2,1)} %bitcast.3) | data formatting | bytes 2621440

commit v9 on v8

--- a/solution.py
+++ b/solution.py
@@ -321,8 +321,6 @@
         )
 
     peers = ((2, opposite), (1, right), (3, left))
-    for k, peer in peers:
-        exchange(k, peer, 0, 0).start()
     hidden = hidden_ref[...].astype(jnp.float32)
     act[...] = (0.5 * hidden * (1.0 + lax.erf(hidden * math.sqrt(0.5)))).astype(jnp.bfloat16)
 
@@ -396,7 +394,7 @@
     gathers[0].forward_near()
     own_start(1)
     each(4, 5, pieces.pass_on)
-    for b, p in ((1, 0), (0, 1), (1, 1), (0, 2), (1, 2)):
+    for b, p in ((0, 0), (1, 0), (0, 1), (1, 1), (0, 2), (1, 2)):
         for k, peer in peers:
             exchange(k, peer, b, p).start()
     gathers[0].forward_far()

time: 155 us -> 152 us (0.981)
  Pallas kernels: 152 us -> 149 us
    pallas_call x1, Pallas kernels: 68.4 us -> 65.3 us  [mix(): pl.pallas_call(mix_kernel, in_specs=[smem, smem, vmem, hbm, hbm, vmem], o...]
where the time goes in v9:
time: 152 us
  Pallas kernels  149 us (98%)
  local copies, waits for them, and re-layouts  2.46 us (2%)
    pallas_call x1, Pallas kernels, attend(): pl.pallas_call(functools.partial(attend_kernel, width=full_width), in_spe...  83.9 us
    pallas_call x1, Pallas kernels, mix(): pl.pallas_call(mix_kernel, in_specs=[smem, smem, vmem, hbm, hbm, vmem], o...  65.3 us

profile of v9, /device:TPU:57, one launch (start us, length us, event | category | flops | bytes accessed | tf_op | source)
XLA Modules:
  0.0 151.7 jit_solution(16464961071119190974)
XLA Ops:
  0.0 65.3 %shard_map.82 = (bf16[1024,1280]{1,0:T(8,128)(2,1)}, f32[8,128]{1,0:T(8,128)}) custom-call(s32[16]{0:T(128)} %start_ref.1, s32[16]{0:T(128)} %count_ref.1, bf16[256,1280]{1,0:T(8,128)(2,1)} %bitcast.4, bf16[1280,5120]{1,0:T(8,128)(2,1)} %w_ref.1, bf16[2,128,5120]{2,1,0:T(8,128)(2,1)} %text_ref.1, f32[1,5120]{1,0:T(1,128)} %bitcast.5), custom_call_target="tpu_custom_call" | custom-call | tf_op jit(solution)/shard_map/pallas_call | solution.py:444
  65.4 83.9 %shard_map.83 = bf16[256,2560]{1,0:T(8,128)(2,1)} custom-call(bf16[1024,1280]{1,0:T(8,128)(2,1)} %get-tuple-element.7.x_ref, f32[8,128]{1,0:T(8,128)} %get-tuple-element.8.square_ref, bf16[1280,1024]{1,0:T(8,128)(2,1)} %wkv_ref.1, bf16[1280,2560]{1,0:T(8,128)(2,1)} %wq_ref.1), custom_call_target="tpu_custom_call" | custom-call | tf_op jit(solution)/shard_map/pallas_call | solution.py:688
  149.3 2.5 %copy.10 = bf16[2,128,2560]{2,1,0:T(8,128)(2,1)} copy(bf16[2,128,2560]{2,1,0:T(8,128)(2,1)} %bitcast.3) | data formatting | bytes 2621440
